TPU v7x, 512 devices: a whole 4x4x16 slice. The times are simulated.
512 devices in a mesh: ifg: 16 (over x, y), pix: 32 (over z, core).
Axes of the slice: x: 4, y: 4, z: 16, core: 2. Of those that a mesh axis runs over, the one named last changes fastest.
Arguments:
- phase: bfloat16 [1200, 49152], P('ifg', 'pix'), may hold values from -8 to 8
- incidence: int32 [2304, 1200], P('ifg'), may hold values from -1 to 1, as said below
- triplet_weight: float32 [2304], P('ifg'), may hold values from 0.3 to 3
- date_pairs: int32 [1200, 2], P('ifg'), may hold values from 0 to 249, as said below
Outputs:
- residual: float32 [2304, 49152], P('ifg', 'pix')
- relative: float32 [49152], P('pix')
- corrected: float32 [1200, 49152], P('ifg', 'pix')
Inputs may be any that keep to these rules, and one draw needn't show every extreme that they name: `incidence`: each row is a closure triplet of three dates a < b < c whose three interferograms all appear in date_pairs: +1 on (a, b) and on (b, c), -1 on (a, c), zeros elsewhere. No two rows are equal. `date_pairs`: interferograms are listed by first date, then by second date; the second date is 1 to 5 dates after the first, and no pair appears twice.
All inputs are finite; a program needn't handle non-finite values.
Results may differ from a plain program's by a relative error of at most 0.013.
Values may be sent and summed in bfloat16 or wider, within the bound.
A program may use at most 64 MiB of HBM per device.

v0:
```python
import jax
import jax.numpy as jnp
from jax import lax
from jax.sharding import PartitionSpec as P


def sent_to_all(value, axis):
    size = lax.axis_size(axis)
    return lax.all_to_all(
        jnp.broadcast_to(value[None], (size, *value.shape)), axis, 0, 0, tiled=True
    )


def of_everyone(value, axis):
    everything = sent_to_all(value, axis)
    return jnp.sum(everything, axis=0)


def in_one(arrays, axis):
    ends = [0]
    for a in arrays:
        ends.append(ends[-1] + a.size)
    so_far = of_everyone(jnp.concatenate([a.ravel() for a in arrays]), axis)
    return tuple((so_far[b:e].reshape(a.shape) for a, b, e in zip(arrays, ends, ends[1:])))


def share_work(every_row, phase_share, groups):
    closure_share = jnp.dot(every_row, phase_share, preferred_element_type=jnp.float32)
    residual_share = jnp.sin(closure_share)
    loss_share = 1.0 - jnp.cos(closure_share)
    wrapped_share = residual_share.astype(jnp.bfloat16)
    block_rows = every_row.shape[0] // groups
    row_blocks = every_row.reshape(groups, block_rows, every_row.shape[1])
    wrap_blocks = wrapped_share.reshape(groups, block_rows, wrapped_share.shape[1])
    partials = lax.dot_general(
        row_blocks, wrap_blocks, (((1,), (1,)), ((0,), (0,))), preferred_element_type=jnp.float32
    )
    correction_share = jnp.sum(partials.astype(jnp.bfloat16).astype(jnp.float32), axis=0)
    return (residual_share, loss_share, correction_share)


def local(phase, incidence, triplet_weight, date_pairs):
    pixel_count = phase.shape[1]
    groups = lax.axis_size("ifg")
    phase_share = lax.all_to_all(phase, "ifg", split_axis=1, concat_axis=0, tiled=True)
    width = incidence.shape[1]
    columns = lax.broadcasted_iota(jnp.int32, incidence.shape, 1)
    plus = incidence == 1
    first_col = jnp.min(jnp.where(plus, columns, width), axis=1)
    second_col = jnp.max(jnp.where(plus, columns, -1), axis=1)
    long_col = jnp.sum(jnp.where(incidence == -1, columns, 0), axis=1)
    triple = jnp.stack([first_col, second_col, long_col], axis=1)
    every_triple = lax.all_gather(triple, "ifg", axis=0, tiled=True)
    all_columns = lax.broadcasted_iota(jnp.int32, (every_triple.shape[0], width), 1)
    rebuilt = (
        (all_columns == every_triple[:, 0:1]).astype(jnp.int32)
        + (all_columns == every_triple[:, 1:2]).astype(jnp.int32)
        - (all_columns == every_triple[:, 2:3]).astype(jnp.int32)
    )
    every_row = rebuilt.astype(jnp.bfloat16)
    residual_share, loss_share, correction_share = share_work(every_row, phase_share, groups)
    residual, losses, correction = (
        lax.all_to_all(residual_share, "ifg", split_axis=0, concat_axis=1, tiled=True),
        lax.all_to_all(loss_share, "ifg", split_axis=0, concat_axis=1, tiled=True),
        lax.all_to_all(correction_share, "ifg", split_axis=0, concat_axis=1, tiled=True),
    )
    local_misfit = jnp.sum(triplet_weight[:, None] * losses, axis=0)
    local_weight = jnp.sum(triplet_weight)
    misfit, total_weight = in_one((local_misfit, local_weight), "ifg")
    score = misfit / total_weight
    all_pixels = pixel_count * lax.axis_size("pix")
    mean_score = of_everyone(jnp.sum(score), "pix") / all_pixels
    relative = score / mean_score
    span = (date_pairs[:, 1] - date_pairs[:, 0]).astype(jnp.float32)
    corrected = phase.astype(jnp.float32) - correction / (2.0 + span)[:, None]
    return (residual, relative, corrected)


def solution(mesh):
    return jax.shard_map(
        local,
        mesh=mesh,
        in_specs=(P("ifg", "pix"), P("ifg", None), P("ifg"), P("ifg", None)),
        out_specs=(P("ifg", "pix"), P("pix"), P("ifg", "pix")),
        check_vma=False,
    )
```

profile of v0, /device:TPU:1, one launch (start us, length us, event | category | flops | bytes accessed | tf_op | source)
XLA Modules:
  0.0 140.5 jit_solution(13953332700943119166)
XLA Ops:
  0.6 1.3 all_to_all.60
  1.9 0.8 copy.43
  2.7 7.6 %all-to-all-start = ((bf16[75,16,96]{2,0,1:T(8,128)(2,1)}), bf16[75,16,96]{2,0,1:T(8,128)(2,1)S(1)}, u32[]{:S(2)}, u32[]{:S(2)}) async-start(bf16[75,16,96]{2,0,1:T(8,128)(2,1)} %copy.43), calls=%async_computation | async-start | bytes 655360 | tf_op jit(solution)/shard_map/all_to_all | solution.py:45
  10.8 19.0 %all-gather = s32[16,144,3]{1,2,0:T(4,128)S(1)} all-gather(s32[1,144,3]{1,2,0:T(4,128)S(1)} %add_bitcast_fusion), channel_id=1, replica_groups=mesh['ifg'=16,'pix'=32] {'ifg'}, dimensions={0}, use_global_device_ids=true | all-gather | bytes 29376 | tf_op jit(solution)/shard_map/all_gather | solution.py:53
  30.1 9.8 %cosine_subtract_fusion = (f32[2304,96]{0,1:T(8,128)S(1)}, f32[2304,96]{0,1:T(8,128)S(1)}) fusion(bf16[1200,96]{1,0:T(8,128)(2,1)S(1)} %all_to_all.63, s32[2304]{0:T(1024)S(1)} %get-tuple-element.6, s32[2304]{0:T(1024)S(1)} %get-tuple-element.7, s32[2304]{0:T(1024)S(1)} %get-tuple-element.5), kind=kOutput, calls=%fused_computation.16 | convolution fusion | flops 555945984 | bytes 2027520 | tf_op jit(solution)/shard_map/dot_general | solution.py:28
  39.9 1.4 copy.46
  41.3 4.4 %all-to-all-start.2 = ((f32[16,144,96]{2,1,0:T(8,128)}), f32[16,144,96]{2,1,0:T(8,128)S(1)}, u32[]{:S(2)}, u32[]{:S(2)}) async-start(f32[16,144,96]{2,1,0:T(8,128)} %bitcast.7), calls=%async_computation.2 | async-start | bytes 2359296 | tf_op jit(solution)/shard_map/all_to_all | solution.py:64
  46.3 6.1 %convert_reduce_fusion = f32[1200,96]{0,1:T(8,128)S(1)} fusion(bf16[16,144,96]{2,1,0:T(8,128)(2,1)S(1)} %bitcast.22, s32[16,144]{1,0:T(8,128)S(1)} %eq.79, s32[16,144]{1,0:T(8,128)S(1)} %eq.76, s32[16,144]{1,0:T(8,128)S(1)} %eq.73), kind=kOutput, calls=%fused_computation.8 | convolution fusion | flops 561139200 | bytes 930816 | tf_op jit(solution)/shard_map/dot_general | solution.py:35
  52.7 0.9 all_to_all.72
  53.5 4.7 %all-to-all-done.2 = f32[16,144,96]{2,1,0:T(8,128)S(1)} async-done(((f32[16,144,96]{2,1,0:T(8,128)}), f32[16,144,96]{2,1,0:T(8,128)S(1)}, u32[]{:S(2)}, u32[]{:S(2)}) %all-to-all-start.2) | async-done | bytes 884768 | tf_op jit(solution)/shard_map/all_to_all | solution.py:64
  58.2 3.6 %all-to-all-start.5 = ((f32[16,75,96]{2,1,0:T(8,128)}), f32[16,75,96]{2,1,0:T(8,128)S(1)}, u32[]{:S(2)}, u32[]{:S(2)}) async-start(f32[16,75,96]{2,1,0:T(8,128)} %all_to_all.72), calls=%async_computation.5 | async-start | bytes 1310720 | tf_op jit(solution)/shard_map/all_to_all | solution.py:65
  63.4 8.1 %all-to-all-done.5 = f32[16,75,96]{2,1,0:T(8,128)S(1)} async-done(((f32[16,75,96]{2,1,0:T(8,128)}), f32[16,75,96]{2,1,0:T(8,128)S(1)}, u32[]{:S(2)}, u32[]{:S(2)}) %all-to-all-start.5) | async-done | bytes 460832 | tf_op jit(solution)/shard_map/all_to_all | solution.py:65
  72.1 3.5 %all-to-all-start.3 = ((f32[16,1,1537]{2,1,0:T(1,128)}), f32[16,1,1537]{2,1,0:T(1,128)S(1)}, u32[]{:S(2)}, u32[]{:S(2)}) async-start(f32[16,1,1537]{2,1,0:T(1,128)} %broadcast_in_dim.27), calls=%async_computation.3 | async-start | bytes 212992 | tf_op jit(solution)/shard_map/all_to_all | solution.py:9
  75.6 1.4 copy.44
  77.0 5.2 %all-to-all-done.3 = f32[16,1,1537]{2,1,0:T(1,128)S(1)} async-done(((f32[16,1,1537]{2,1,0:T(1,128)}), f32[16,1,1537]{2,1,0:T(1,128)S(1)}, u32[]{:S(2)}, u32[]{:S(2)}) %all-to-all-start.3) | async-done | bytes 98400 | tf_op jit(solution)/shard_map/all_to_all | solution.py:9
  82.2 3.8 %all-to-all-start.1 = ((f32[16,144,96]{2,1,0:T(8,128)}), f32[16,144,96]{2,1,0:T(8,128)S(1)}, u32[]{:S(2)}, u32[]{:S(2)}) async-start(f32[16,144,96]{2,1,0:T(8,128)} %bitcast.5), calls=%async_computation.1 | async-start | bytes 2359296 | tf_op jit(solution)/shard_map/all_to_all | solution.py:63
  87.2 1.2 divide_reduce_fusion
  88.5 10.6 %all-to-all-done.1 = f32[16,144,96]{2,1,0:T(8,128)S(1)} async-done(((f32[16,144,96]{2,1,0:T(8,128)}), f32[16,144,96]{2,1,0:T(8,128)S(1)}, u32[]{:S(2)}, u32[]{:S(2)}) %all-to-all-start.1) | async-done | bytes 884768 | tf_op jit(solution)/shard_map/all_to_all | solution.py:63
  99.1 1.2 broadcast_in_dim.28
  100.3 25.7 %all-to-all-start.4 = ((f32[32,1,1]{2,1,0:T(1,128)}), f32[32,1,1]{2,1,0:T(1,128)S(1)}, u32[]{:S(2)}, u32[]{:S(2)}) async-start(f32[32,1,1]{2,1,0:T(1,128)} %broadcast_in_dim.28), calls=%async_computation.4 | async-start | bytes 32768 | tf_op jit(solution)/shard_map/all_to_all | solution.py:9
  126.1 0.9 divide_subtract_fusion
  127.4 1.4 all_to_all.67
  128.8 9.1 %all-to-all-done.4 = f32[32,1,1]{2,1,0:T(1,128)S(1)} async-done(((f32[32,1,1]{2,1,0:T(1,128)}), f32[32,1,1]{2,1,0:T(1,128)S(1)}, u32[]{:S(2)}, u32[]{:S(2)}) %all-to-all-start.4) | async-done | bytes 160 | tf_op jit(solution)/shard_map/all_to_all | solution.py:9
  137.8 0.7 reduce_sum.71
  (33 shorter events, 5.9 us)
Async XLA Ops:
  0.6 9.7 %copy-start.1 = (s32[144,1200]{1,0:T(8,128)S(1)}, s32[144,1200]{1,0:T(8,128)}, u32[]{:S(2)}) copy-start(s32[144,1200]{1,0:T(8,128)} %param.5) | copy-start | bytes 2073604
  2.7 27.2 %all-to-all-start = ((bf16[75,16,96]{2,0,1:T(8,128)(2,1)}), bf16[75,16,96]{2,0,1:T(8,128)(2,1)S(1)}, u32[]{:S(2)}, u32[]{:S(2)}) async-start(bf16[75,16,96]{2,0,1:T(8,128)(2,1)} %copy.43), calls=%async_computation | async-start | bytes 655360 | tf_op jit(solution)/shard_map/all_to_all | solution.py:45
  41.3 16.9 %all-to-all-start.2 = ((f32[16,144,96]{2,1,0:T(8,128)}), f32[16,144,96]{2,1,0:T(8,128)S(1)}, u32[]{:S(2)}, u32[]{:S(2)}) async-start(f32[16,144,96]{2,1,0:T(8,128)} %bitcast.7), calls=%async_computation.2 | async-start | bytes 2359296 | tf_op jit(solution)/shard_map/all_to_all | solution.py:64
  52.6 9.2 %copy-start.2 = (f32[144]{0:T(256)S(1)}, f32[144]{0:T(256)}, u32[]{:S(2)}) copy-start(f32[144]{0:T(256)} %param.6) | copy-start | bytes 1732
  58.2 13.2 %all-to-all-start.5 = ((f32[16,75,96]{2,1,0:T(8,128)}), f32[16,75,96]{2,1,0:T(8,128)S(1)}, u32[]{:S(2)}, u32[]{:S(2)}) async-start(f32[16,75,96]{2,1,0:T(8,128)} %all_to_all.72), calls=%async_computation.5 | async-start | bytes 1310720 | tf_op jit(solution)/shard_map/all_to_all | solution.py:65
  72.1 10.1 %all-to-all-start.3 = ((f32[16,1,1537]{2,1,0:T(1,128)}), f32[16,1,1537]{2,1,0:T(1,128)S(1)}, u32[]{:S(2)}, u32[]{:S(2)}) async-start(f32[16,1,1537]{2,1,0:T(1,128)} %broadcast_in_dim.27), calls=%async_computation.3 | async-start | bytes 212992 | tf_op jit(solution)/shard_map/all_to_all | solution.py:9
  82.2 3.8 %copy-start.3 = (s32[75,2]{0,1:T(2,128)S(1)}, s32[75,2]{0,1:T(2,128)}, u32[]{:S(2)}) copy-start(s32[75,2]{0,1:T(2,128)} %param.7) | copy-start | bytes 1804
  82.2 16.9 %all-to-all-start.1 = ((f32[16,144,96]{2,1,0:T(8,128)}), f32[16,144,96]{2,1,0:T(8,128)S(1)}, u32[]{:S(2)}, u32[]{:S(2)}) async-start(f32[16,144,96]{2,1,0:T(8,128)} %bitcast.5), calls=%async_computation.1 | async-start | bytes 2359296 | tf_op jit(solution)/shard_map/all_to_all | solution.py:63
  86.1 40.0 %copy-start = (bf16[75,1536]{1,0:T(8,128)(2,1)S(1)}, bf16[75,1536]{1,0:T(8,128)(2,1)}, u32[]{:S(2)}) copy-start(bf16[75,1536]{1,0:T(8,128)(2,1)} %param.4) | copy-start | bytes 691204
  100.3 37.5 %all-to-all-start.4 = ((f32[32,1,1]{2,1,0:T(1,128)}), f32[32,1,1]{2,1,0:T(1,128)S(1)}, u32[]{:S(2)}, u32[]{:S(2)}) async-start(f32[32,1,1]{2,1,0:T(1,128)} %broadcast_in_dim.28), calls=%async_computation.4 | async-start | bytes 32768 | tf_op jit(solution)/shard_map/all_to_all | solution.py:9
where the time goes:
time: 141 us; the launch traced here: 140 us
  starting transfers between devices  48.7 us (35%)
  waiting for transfers between devices  37.6 us (27%)
  blocking collectives  19 us (13%)
  matrix products  15.9 us (11%)
  local copies, waits for them, and re-layouts  11.6 us (8%)
  other arithmetic  5.54 us (4%)
  between operations  2.21 us (2%)
    all_to_all x2, starting transfers between devices, sent_to_all(): lax.all_to_all(jnp.broadcast_to(value[None], (size, *value.shape)), axis,...  29.2 us
    all_gather x1, blocking collectives, local(): every_triple = lax.all_gather(triple, 'ifg', axis=0, tiled=True)  19 us
    all_to_all x2, waiting for transfers between devices, sent_to_all(): lax.all_to_all(jnp.broadcast_to(value[None], (size, *value.shape)), axis,...  14.3 us
    all_to_all x1, waiting for transfers between devices, local(): lax.all_to_all(residual_share, 'ifg', split_axis=0, concat_axis=1, tiled=...  10.6 us
    dot_general x1, matrix products, share_work(): jnp.dot(every_row, phase_share, preferred_element_type=jnp.float32)  9.78 us
    all_to_all x1, waiting for transfers between devices, local(): lax.all_to_all(correction_share, 'ifg', split_axis=0, concat_axis=1, tile...  8.06 us
    all_to_all x1, starting transfers between devices, local(): lax.all_to_all(phase, 'ifg', split_axis=1, concat_axis=0, tiled=True)  7.57 us
    dot_general x1, matrix products, share_work(): lax.dot_general(row_blocks, wrap_blocks, (((1,), (1,)), ((0,), (0,))), pr...  6.07 us
  transfers between devices with their start and end apart: 6, of which 5 were waited for; matrix products, arithmetic and copies ran while one was open for 10% of the time, Pallas kernels for 0%

commit v1 on v0

v1 whole, which is shorter than its diff:
```python
import jax
import jax.numpy as jnp
from jax import lax
from jax.experimental import pallas as pl
from jax.experimental.pallas import tpu as pltpu
from jax.sharding import PartitionSpec as P

GROUP = 16
LANES = 128
INV_PI = 0.3183098861837907
PI_HI = 3.140625
PI_LO = 9.676535897932e-4
SIN = (-0.16666657096162138, 0.008333017284575896, -0.00019806614761156636, 2.6000538932920348e-06)
COS = (0.4999999954954239, -0.04166664072751474, 0.0013888403501702445, -2.476188593339371e-05, 2.607710003258223e-07)


def poly(coefs, z):
    out = jnp.full_like(z, coefs[-1])
    for c in coefs[-2::-1]:
        out = out * z + c
    return out


def sin_and_loss(x):
    k = jnp.floor(x * INV_PI + 0.5)
    r = (x - k * PI_HI) - k * PI_LO
    half = k * 0.5
    odd2 = (half - jnp.floor(half)) * 4.0
    sign = 1.0 - odd2
    z = r * r
    sine = sign * (r + (r * z) * poly(SIN, z))
    loss = odd2 + sign * (z * poly(COS, z))
    return sine, loss


def rank_of(device, core):
    return lax.rem(lax.rem(device, 4) - device // 4 - 2 * core + 7, 4)


def kernel(
    phase_ref, idx_ref, res_ref, cor_ref, score_ref,
    padded, ph, pht, idxs, tiles, inct, iota, wb, cb, acc, row,
    idx_s, idx_r, ph_s, ph_r, res_s, res_r, lef_s, lef_r, cor_s, cor_r, sc_s, sc_r,
):
    me = lax.axis_index("ifg")
    core = lax.rem(lax.axis_index("pix"), 2)
    rank = rank_of(me, core)
    active = rank < 3
    share = 3 * (me // 4) + rank
    my_lanes = pl.ds(pl.multiple_of(share * LANES, LANES), LANES)
    rows = phase_ref.shape[0]
    depth = padded.shape[0]

    barrier = pltpu.get_barrier_semaphore()

    @pl.loop(1, GROUP)
    def _(k):
        pl.semaphore_signal(barrier, inc=1, device_id={"ifg": lax.rem(me + k, GROUP)}, device_id_type=pl.DeviceIdType.MESH)

    padded[...] = jnp.zeros_like(padded)
    padded[0:rows, :] = phase_ref[...]
    iota[...] = lax.broadcasted_iota(jnp.int32, iota.shape, 0).astype(jnp.float32).astype(jnp.bfloat16)
    acc[...] = jnp.zeros_like(acc)

    pl.semaphore_wait(barrier, GROUP - 1)

    def put(src, dst, send, recv, device):
        @pl.when(device != me)
        def _():
            pltpu.make_async_remote_copy(
                src_ref=src, dst_ref=dst, send_sem=send, recv_sem=recv,
                device_id={"ifg": device}, device_id_type=pl.DeviceIdType.MESH,
            ).start()

        @pl.when(device == me)
        def _():
            pltpu.make_async_copy(src, dst, recv).start()

    def took(ref, sem):
        pltpu.make_async_copy(ref, ref, sem).wait()

    def to_shares(body):
        @pl.loop(0, GROUP)
        def _(k):
            device = lax.rem(me + k, GROUP)
            their = rank_of(device, core)

            @pl.when(their < 3)
            def _():
                body(device, pl.multiple_of((3 * (device // 4) + their) * LANES, LANES))

    to_shares(lambda d, at: put(idx_ref, idxs.at[me], idx_s.at[d], idx_r.at[me], d))
    to_shares(lambda d, at: put(padded.at[:, pl.ds(at, LANES)], ph.at[me], ph_s.at[d], ph_r.at[me], d))

    @pl.when(active)
    def _():
        @pl.loop(0, GROUP)
        def _(d):
            took(idxs.at[d], idx_r.at[d])

        for p in range(GROUP // 2):
            tiles[p, :, 0:LANES] = idxs[2 * p, :, 0:LANES]
            tiles[p, :, LANES:] = idxs[2 * p + 1, :, 0:LANES]
        for q in range(2):
            rest = idxs[8 * q, :, LANES:]
            for i in range(1, 8):
                rest = rest + idxs[8 * q + i, :, LANES:]
            tiles[GROUP // 2, :, q * LANES : (q + 1) * LANES] = rest

        @pl.loop(0, GROUP // 2 + 1)
        def _(p):
            t = tiles[p]

            @pl.loop(0, GROUP)
            def _(b):
                rel = (t - lax.convert_element_type(b * depth, jnp.float32)).astype(jnp.bfloat16)
                at = iota[...]
                one = jnp.ones(at.shape, jnp.bfloat16)
                both = jnp.logical_or(at == rel[0:1], at == rel[1:2])
                signed = jnp.where(at == rel[2:3], -one, jnp.where(both, one, jnp.zeros_like(one)))
                inct[p, pl.ds(pl.multiple_of(b * depth, depth), depth), :] = signed

        for half in range(2):
            for d in range(8 * half, 8 * half + 8):
                took(ph.at[d], ph_r.at[d])
            block = ph[8 * half : 8 * half + 8].reshape(8 * depth, LANES)
            pht[:, 8 * depth * half : 8 * depth * (half + 1)] = jnp.transpose(block.astype(jnp.float32)).astype(jnp.bfloat16)

        def closures(p):
            closure = jnp.dot(pht[...], inct[p], preferred_element_type=jnp.float32)
            sine, loss = sin_and_loss(closure)
            acc[...] += loss * tiles[p, 3:4, :]
            wb[p] = jnp.transpose(sine).astype(jnp.bfloat16)

        @pl.loop(0, GROUP // 2)
        def _(j):
            p = lax.rem(me // 2 + j, GROUP // 2)
            closures(p)
            for q in range(2):
                d = 2 * p + q
                put(wb.at[p, pl.ds(q * LANES, LANES)], res_ref.at[pl.ds(0, LANES), my_lanes], res_s.at[d], res_r.at[share], d)

        closures(GROUP // 2)

        @pl.loop(0, GROUP)
        def _(k):
            d = lax.rem(me + k, GROUP)
            put(
                wb.at[GROUP // 2, pl.ds(pl.multiple_of(16 * d, 16), 16)],
                res_ref.at[pl.ds(LANES, 16), my_lanes], lef_s.at[d], lef_r.at[share], d,
            )

        total = tiles[0, 3:4, :]
        for p in range(1, GROUP // 2 + 1):
            total = total + tiles[p, 3:4, :]
        both = acc[:, 0:LANES] + acc[:, LANES:]
        misfit = jnp.sum(jnp.transpose(both), axis=0, keepdims=True)
        row[...] = misfit / jnp.sum(total, axis=1, keepdims=True)

        @pl.loop(0, 4)
        def _(j):
            c = lax.rem(me // 4 + j, 4)
            at = pl.ds(pl.multiple_of(c * 4 * depth, 4 * depth), 4 * depth)
            corr = jnp.zeros((4 * depth, LANES), jnp.float32)
            for p in range(GROUP // 2 + 1):
                corr = corr + jnp.dot(inct[p, at, :], wb[p], preferred_element_type=jnp.float32)
            cb[pl.ds(4 * c, 4)] = corr.astype(jnp.bfloat16).reshape(4, depth, LANES)
            for q in range(4):
                d = 4 * c + q
                put(cb.at[d], cor_ref.at[:, my_lanes], cor_s.at[d], cor_r.at[share], d)

        @pl.loop(0, GROUP)
        def _(k):
            d = lax.rem(me + k, GROUP)
            put(row, score_ref.at[share], sc_s.at[d], sc_r.at[share], d)

    @pl.loop(0, 12)
    def _(s):
        lanes = pl.ds(pl.multiple_of(s * LANES, LANES), LANES)
        took(res_ref.at[pl.ds(0, LANES), lanes], res_r.at[s])
        took(res_ref.at[pl.ds(LANES, 16), lanes], lef_r.at[s])
        took(cor_ref.at[:, lanes], cor_r.at[s])
        took(score_ref.at[s], sc_r.at[s])

    @pl.loop(1, GROUP)
    def _(k):
        d = lax.rem(me + k, GROUP)

        @pl.when(rank_of(d, core) < 3)
        def _():
            took(idxs.at[0], idx_s.at[d])
            took(ph.at[0], ph_s.at[d])

        @pl.when(active)
        def _():
            took(wb.at[0, pl.ds(0, LANES)], res_s.at[d])
            took(wb.at[0, pl.ds(0, 16)], lef_s.at[d])
            took(cb.at[0], cor_s.at[d])
            took(row, sc_s.at[d])


def local(phase, incidence, triplet_weight, date_pairs):
    rows, pixel_count = phase.shape
    depth = -(-rows // 16) * 16
    triplets, width = incidence.shape
    me = lax.axis_index("ifg")
    columns = lax.broadcasted_iota(jnp.int32, incidence.shape, 1)
    columns = (columns + (columns // rows) * (depth - rows)).astype(jnp.float32)
    plus = incidence == 1
    first = jnp.min(jnp.where(plus, columns, 4096.0), axis=1)
    second = jnp.max(jnp.where(plus, columns, -1.0), axis=1)
    long = jnp.sum(jnp.where(incidence == -1, columns, 0.0), axis=1)
    four = jnp.stack([first, second, long, triplet_weight])
    lane = lax.broadcasted_iota(jnp.int32, (4, LANES), 1)
    rest = jnp.where(lane // 16 == lax.rem(me, 8), jnp.tile(four[:, LANES:], (1, 8)), 0.0)
    idx = jnp.pad(jnp.concatenate([four[:, :LANES], rest], axis=1), ((0, 4), (0, 0)))

    shares = pixel_count // LANES
    pairs = GROUP // 2 + 1
    vmem = pl.BlockSpec(memory_space=pltpu.VMEM)
    sems = [pltpu.SemaphoreType.DMA((GROUP,))] * 12
    residual, correction, score = pl.pallas_call(
        kernel,
        out_shape=(
            jax.ShapeDtypeStruct((triplets, pixel_count), jnp.bfloat16),
            jax.ShapeDtypeStruct((depth, pixel_count), jnp.bfloat16),
            jax.ShapeDtypeStruct((shares, 1, LANES), jnp.float32),
        ),
        in_specs=[vmem] * 2,
        out_specs=[vmem] * 3,
        scratch_shapes=[
            pltpu.VMEM((depth, pixel_count), jnp.bfloat16),
            pltpu.VMEM((GROUP, depth, LANES), jnp.bfloat16),
            pltpu.VMEM((LANES, GROUP * depth), jnp.bfloat16),
            pltpu.VMEM((GROUP, 8, 2 * LANES), jnp.float32),
            pltpu.VMEM((pairs, 8, 2 * LANES), jnp.float32),
            pltpu.VMEM((pairs, GROUP * depth, 2 * LANES), jnp.bfloat16),
            pltpu.VMEM((depth, 2 * LANES), jnp.bfloat16),
            pltpu.VMEM((pairs, 2 * LANES, LANES), jnp.bfloat16),
            pltpu.VMEM((GROUP, depth, LANES), jnp.bfloat16),
            pltpu.VMEM((LANES, 2 * LANES), jnp.float32),
            pltpu.VMEM((1, LANES), jnp.float32),
            *sems,
        ],
        compiler_params=pltpu.CompilerParams(collective_id=0, has_side_effects=True),
    )(phase, idx)

    score = score.reshape(pixel_count)
    all_pixels = pixel_count * lax.axis_size("pix")
    relative = score / (lax.psum(jnp.sum(score), "pix") / all_pixels)
    span = (date_pairs[:, 1] - date_pairs[:, 0]).astype(jnp.float32)
    corrected = phase.astype(jnp.float32) - correction[:rows].astype(jnp.float32) / (2.0 + span)[:, None]
    return (residual.astype(jnp.float32), relative, corrected)


def solution(mesh):
    return jax.shard_map(
        local,
        mesh=mesh,
        in_specs=(P("ifg", "pix"), P("ifg", None), P("ifg"), P("ifg", None)),
        out_specs=(P("ifg", "pix"), P("pix"), P("ifg", "pix")),
        check_vma=False,
    )
```

time: 141 us -> 97.1 us (0.69)
  starting transfers between devices: 48.7 us -> 0 us
  waiting for transfers between devices: 37.6 us -> 0 us
  blocking collectives: 19 us -> 54.1 us
  Pallas kernels: 0 us -> 31.3 us
  matrix products: 15.9 us -> 0 us
  local copies, waits for them, and re-layouts: 11.6 us -> 2.7 us
  other arithmetic: 5.54 us -> 7.08 us
    psum x0 -> x1, blocking collectives: none -> 54.1 us  [local(): relative = score / (lax.psum(jnp.sum(score), 'pix') / all_pixels)]
    all_to_all x6 -> x0, starting transfers between devices: 48.7 us -> none  [the longest x2 29.2 us: sent_to_all(): lax.all_to_all(jnp.broadcast_to(value[None], (size, *value.shape)), axis,...]
    all_to_all x6 -> x0, waiting for transfers between devices: 37.6 us -> none  [the longest x2 14.3 us: sent_to_all(): lax.all_to_all(jnp.broadcast_to(value[None], (size, *value.shape)), axis,...]
    pallas_call x0 -> x1, Pallas kernels: none -> 31.3 us  [local(): pl.pallas_call(kernel, out_shape=(jax.ShapeDtypeStruct((triplets, pixel_c...]
    all_gather x1 -> x0, blocking collectives: 19 us -> none  [local(): every_triple = lax.all_gather(triple, 'ifg', axis=0, tiled=True)]
    dot_general x2 -> x0, matrix products: 15.9 us -> none  [the longest x1 9.78 us: share_work(): jnp.dot(every_row, phase_share, preferred_element_type=jnp.float32)]
    all_to_all x8 -> x0, local copies, waits for them, and re-layouts: 5.36 us -> none  [the longest x3 2.19 us: local(): lax.all_to_all(phase, 'ifg', split_axis=1, concat_axis=0, tiled=True)]
    convert_element_type x1, other arithmetic: 0.05 us -> 2.07 us  [local(): return (residual.astype(jnp.float32), relative, corrected)]
  transfers between devices with their start and end apart: 6 -> 0, of which waited for: 5 -> 0; matrix products, arithmetic and copies ran while one was open for 10% -> 0% of each run, Pallas kernels for 0% -> 0%
where the time goes in v1:
time: 97.1 us; the launch traced here: 96.5 us
  blocking collectives  54.1 us (56%)
  Pallas kernels  31.3 us (32%)
  other arithmetic  7.08 us (7%)
  local copies, waits for them, and re-layouts  2.7 us (3%)
  between operations  1.36 us (1%)
    psum x1, blocking collectives, local(): relative = score / (lax.psum(jnp.sum(score), 'pix') / all_pixels)  54.1 us
    pallas_call x1, Pallas kernels, local(): pl.pallas_call(kernel, out_shape=(jax.ShapeDtypeStruct((triplets, pixel_c...  31.3 us
    convert_element_type x1, other arithmetic, local(): return (residual.astype(jnp.float32), relative, corrected)  2.07 us

profile of v1, /device:TPU:1, one launch (start us, length us, event | category | flops | bytes accessed | tf_op | source)
XLA Modules:
  0.0 96.5 jit_solution(5483686045859401684)
XLA Ops:
  0.6 0.0 copy-start.5
  0.6 0.7 copy-done.5
  1.4 1.4 %select_reduce_fusion.2 = (f32[144]{0:T(256)S(1)}, f32[144]{0:T(256)S(1)}, f32[144]{0:T(256)S(1)}) fusion(s32[1200]{0:T(1024)S(1)} %get-tuple-element.12, s32[1200]{0:T(1024)S(1)} %get-tuple-element.13, pred[1200]{0:T(1024)(128)(4,1)S(1)} %fusion.2, s32[144,1200]{1,0:T(8,128)} %param.5), kind=kLoop, calls=%fused_computation.2 | loop fusion | flops 2073168 | bytes 703728 | tf_op jit(solution)/shard_map/reduce_min | solution.py:210
  2.8 0.0 copy-start.4
  2.8 0.7 copy-done.4
  3.5 0.0 copy-start.3
  3.5 0.6 copy-done.3
  4.1 0.1 tile.10
  4.2 0.0 slice-start
  4.2 0.7 slice-done
  4.9 0.6 select_maximum_fusion.idx_ref
  5.5 31.3 %shard_map.67 = (bf16[144,1536]{1,0:T(8,128)(2,1)}, bf16[80,1536]{1,0:T(8,128)(2,1)}, f32[12,1,128]{2,1,0:T(1,128)}) custom-call(bf16[75,1536]{1,0:T(8,128)(2,1)} %phase_ref.1, f32[8,256]{1,0:T(8,128)} %select_maximum_fusion.idx_ref), custom_call_target="tpu_custom_call" | custom-call | tf_op jit(solution)/shard_map/pallas_call | solution.py:222
  36.8 0.0 copy-start.2
  36.8 1.4 %reduce_sum.19 = f32[]{:T(128)} reduce(f32[12,1,128]{2,1,0:T(1,128)} %get-tuple-element.7, f32[]{:T(128)} %constant.51.clone.1), dimensions={0,1,2}, to_apply=%region_3.4 | reduce | flops 1535 | bytes 6152 | tf_op jit(solution)/shard_map/reduce_sum | solution.py:250
  38.2 54.1 %psum.7 = f32[]{:T(128)} all-reduce(f32[]{:T(128)} %reduce_sum.19), channel_id=1, replica_groups=mesh['ifg'=16,'pix'=32] {'pix'}, use_global_device_ids=true, to_apply=%region_4.5 | all-reduce | flops 1 | bytes 8 | tf_op jit(solution)/shard_map/psum | solution.py:250
  92.9 0.0 copy-done.2
  92.9 0.6 divide_reduce_fusion
  93.5 0.0 copy-start
  93.5 0.0 copy-start.1
  93.5 2.1 %convert_element_type.23 = f32[144,1536]{1,0:T(8,128)} convert(bf16[144,1536]{1,0:T(8,128)(2,1)} %get-tuple-element.6) | non-fusion elementwise | flops 221184 | bytes 1327104 | tf_op jit(solution)/shard_map/convert_element_type | solution.py:253
  95.6 0.0 copy-done
  95.6 0.0 copy-done.1
  95.6 0.9 divide_subtract_fusion
  (9 shorter events, 0.1 us)
Async XLA Ops:
  0.6 0.7 copy-start.5
  2.8 0.7 copy-start.4
  3.5 0.6 copy-start.3
  4.2 0.7 slice-start
  36.8 56.1 %copy-start.2 = (f32[12,1,128]{2,1,0:T(1,128)S(1)}, f32[12,1,128]{2,1,0:T(1,128)}, u32[]{:S(2)}) copy-start(f32[12,1,128]{2,1,0:T(1,128)} %get-tuple-element.7) | copy-start | bytes 18436
  93.5 2.1 %copy-start = (bf16[75,1536]{1,0:T(8,128)(2,1)S(1)}, bf16[75,1536]{1,0:T(8,128)(2,1)}, u32[]{:S(2)}) copy-start(bf16[75,1536]{1,0:T(8,128)(2,1)} %phase_ref.1) | copy-start | bytes 691204
  93.5 2.1 %copy-start.1 = (bf16[80,1536]{1,0:T(8,128)(2,1)S(1)}, bf16[80,1536]{1,0:T(8,128)(2,1)}, u32[]{:S(2)}) copy-start(bf16[80,1536]{1,0:T(8,128)(2,1)} %get-tuple-element.8) | copy-start | bytes 737284

commit v2 on v1

--- a/solution.py
+++ b/solution.py
@@ -1,3 +1,5 @@
+import functools
+
 import jax
 import jax.numpy as jnp
 from jax import lax
@@ -38,12 +40,15 @@
 
 
 def kernel(
-    phase_ref, idx_ref, res_ref, cor_ref, score_ref,
-    padded, ph, pht, idxs, tiles, inct, iota, wb, cb, acc, row,
-    idx_s, idx_r, ph_s, ph_r, res_s, res_r, lef_s, lef_r, cor_s, cor_r, sc_s, sc_r,
+    all_pixels,
+    phase_ref, inc_hbm, weight_ref, res_ref, cor_ref, rel_ref,
+    inc, idx, rest16, wrow, padded, ph, pht, idxs, tiles, inct, iota, wb, cb, acc, scores, fin_out, fin,
+    inc_sem, idx_s, idx_r, ph_s, ph_r, res_s, res_r, lef_s, lef_r, cor_s, cor_r, fin_s, fin_r, pix_s, pix_r,
+    near1, near2, near4,
 ):
     me = lax.axis_index("ifg")
-    core = lax.rem(lax.axis_index("pix"), 2)
+    pix = lax.axis_index("pix")
+    core = lax.rem(pix, 2)
     rank = rank_of(me, core)
     active = rank < 3
     share = 3 * (me // 4) + rank
@@ -51,18 +56,63 @@
     rows = phase_ref.shape[0]
     depth = padded.shape[0]
 
+    pixes = scores.shape[0]
+
     barrier = pltpu.get_barrier_semaphore()
 
-    @pl.loop(1, GROUP)
-    def _(k):
+    def tell_group(k):
         pl.semaphore_signal(barrier, inc=1, device_id={"ifg": lax.rem(me + k, GROUP)}, device_id_type=pl.DeviceIdType.MESH)
+
+    def tell_pix(sem, other):
+        pl.semaphore_signal(sem, inc=1, device_id={"pix": lax.rem(other, pixes)}, device_id_type=pl.DeviceIdType.MESH)
+
+    def tell_along_z(sem, distance):
+        tell_pix(sem, pix + 2 * distance)
+        tell_pix(sem, pix + pixes - 2 * distance)
+
+    pl.loop(1, GROUP)(tell_group)
+    across = 2 * (pix // 2) + 1 - core
+    tell_pix(barrier, across)
+    tell_along_z(barrier, 1)
+    tell_pix(barrier, across + 2)
+    tell_pix(barrier, across + pixes - 2)
+    read_inc = pltpu.make_async_copy(inc_hbm, inc, inc_sem)
+    read_inc.start()
 
     padded[...] = jnp.zeros_like(padded)
     padded[0:rows, :] = phase_ref[...]
     iota[...] = lax.broadcasted_iota(jnp.int32, iota.shape, 0).astype(jnp.float32).astype(jnp.bfloat16)
     acc[...] = jnp.zeros_like(acc)
 
-    pl.semaphore_wait(barrier, GROUP - 1)
+    scores[pix] = jnp.zeros(scores.shape[1:], scores.dtype)
+    fin_out[...] = jnp.zeros_like(fin_out)
+    wrow[...] = jnp.zeros_like(wrow)
+    wrow[0:1, 0 : weight_ref.shape[1]] = weight_ref[...]
+    rest16[...] = jnp.zeros_like(rest16)
+
+    read_inc.wait()
+    width = inc.shape[1]
+    column = lax.broadcasted_iota(jnp.int32, (1, width), 1).astype(jnp.float32)
+    column = column + jnp.floor((column + 0.5) * (1.0 / rows)) * (depth - rows)
+    value = inc[...]
+    plus = value == 1
+    first = jnp.min(jnp.where(plus, column, 4096.0), axis=1, keepdims=True)
+    second = jnp.max(jnp.where(plus, column, -1.0), axis=1, keepdims=True)
+    long = jnp.sum(jnp.where(value == -1, column, 0.0), axis=1, keepdims=True)
+    lane = lax.broadcasted_iota(jnp.int32, (inc.shape[0], LANES), 1)
+    three = jnp.where(lane == 0, first, jnp.where(lane == 1, second, long))
+    spot = 16 * lax.rem(me, 8)
+    rest16[pl.ds(pl.multiple_of(spot, 16), 16), :] = three[LANES:]
+    line = lax.broadcasted_iota(jnp.int32, (8, LANES), 0)
+    for q, t, w in (
+        (0, three[:LANES], wrow[:, :LANES]),
+        (1, rest16[...], pltpu.roll(wrow[:, LANES:], spot, 1)),
+    ):
+        t = jnp.where(line < 3, jnp.transpose(t)[0:8], 0.0)
+        idx[:, q * LANES : (q + 1) * LANES] = jnp.where(line == 3, jnp.broadcast_to(w[0:1], t.shape), t)
+
+    pl.semaphore_wait(barrier, GROUP + 4)
+    tell_along_z(near1, 1)
 
     def put(src, dst, send, recv, device):
         @pl.when(device != me)
@@ -89,7 +139,7 @@
             def _():
                 body(device, pl.multiple_of((3 * (device // 4) + their) * LANES, LANES))
 
-    to_shares(lambda d, at: put(idx_ref, idxs.at[me], idx_s.at[d], idx_r.at[me], d))
+    to_shares(lambda d, at: put(idx, idxs.at[me], idx_s.at[d], idx_r.at[me], d))
     to_shares(lambda d, at: put(padded.at[:, pl.ds(at, LANES)], ph.at[me], ph_s.at[d], ph_r.at[me], d))
 
     @pl.when(active)
@@ -120,12 +170,22 @@
                 signed = jnp.where(at == rel[2:3], -one, jnp.where(both, one, jnp.zeros_like(one)))
                 inct[p, pl.ds(pl.multiple_of(b * depth, depth), depth), :] = signed
 
+    pl.semaphore_wait(near1, 2)
+    tell_along_z(near2, 2)
+
+    @pl.when(active)
+    def _():
         for half in range(2):
             for d in range(8 * half, 8 * half + 8):
                 took(ph.at[d], ph_r.at[d])
             block = ph[8 * half : 8 * half + 8].reshape(8 * depth, LANES)
             pht[:, 8 * depth * half : 8 * depth * (half + 1)] = jnp.transpose(block.astype(jnp.float32)).astype(jnp.bfloat16)
 
+    pl.semaphore_wait(near2, 2)
+    tell_along_z(near4, 4)
+
+    @pl.when(active)
+    def _():
         def closures(p):
             closure = jnp.dot(pht[...], inct[p], preferred_element_type=jnp.float32)
             sine, loss = sin_and_loss(closure)
@@ -155,8 +215,20 @@
             total = total + tiles[p, 3:4, :]
         both = acc[:, 0:LANES] + acc[:, LANES:]
         misfit = jnp.sum(jnp.transpose(both), axis=0, keepdims=True)
-        row[...] = misfit / jnp.sum(total, axis=1, keepdims=True)
-
+        scores[pix] = misfit / jnp.sum(total, axis=1, keepdims=True)
+
+    pl.semaphore_wait(near4, 2)
+
+    @pl.loop(1, pixes)
+    def _(k):
+        other = lax.rem(pix + k, pixes)
+        pltpu.make_async_remote_copy(
+            src_ref=scores.at[pix], dst_ref=scores.at[pix], send_sem=pix_s.at[other], recv_sem=pix_r.at[pix],
+            device_id={"pix": other}, device_id_type=pl.DeviceIdType.MESH,
+        ).start()
+
+    @pl.when(active)
+    def _():
         @pl.loop(0, 4)
         def _(j):
             c = lax.rem(me // 4 + j, 4)
@@ -169,10 +241,19 @@
                 d = 4 * c + q
                 put(cb.at[d], cor_ref.at[:, my_lanes], cor_s.at[d], cor_r.at[share], d)
 
-        @pl.loop(0, GROUP)
-        def _(k):
-            d = lax.rem(me + k, GROUP)
-            put(row, score_ref.at[share], sc_s.at[d], sc_r.at[share], d)
+    @pl.loop(1, pixes)
+    def _(k):
+        other = lax.rem(pix + k, pixes)
+        took(scores.at[other], pix_r.at[other])
+
+    fin_out[0:1] = scores[pix]
+    fin_out[1:2] = jnp.sum(scores[...], axis=0)
+    slot = jnp.where(active, share, 12 + me // 4)
+
+    @pl.loop(0, GROUP)
+    def _(k):
+        d = lax.rem(me + k, GROUP)
+        put(fin_out, fin.at[slot], fin_s.at[d], fin_r.at[slot], d)
 
     @pl.loop(0, 12)
     def _(s):
@@ -180,11 +261,25 @@
         took(res_ref.at[pl.ds(0, LANES), lanes], res_r.at[s])
         took(res_ref.at[pl.ds(LANES, 16), lanes], lef_r.at[s])
         took(cor_ref.at[:, lanes], cor_r.at[s])
-        took(score_ref.at[s], sc_r.at[s])
+
+    @pl.loop(0, GROUP)
+    def _(s):
+        took(fin.at[s], fin_r.at[s])
+
+    everything = jnp.sum(jnp.sum(fin[...], axis=0)[1:2], axis=1, keepdims=True)
+    for s in range(12):
+        rel_ref[s] = fin[s, 0:1] / (everything / all_pixels)
+
+    @pl.loop(1, pixes)
+    def _(k):
+        other = lax.rem(pix + k, pixes)
+        took(scores.at[pix], pix_s.at[other])
 
     @pl.loop(1, GROUP)
     def _(k):
         d = lax.rem(me + k, GROUP)
+
+        took(fin_out, fin_s.at[d])
 
         @pl.when(rank_of(d, core) < 3)
         def _():
@@ -196,39 +291,31 @@
             took(wb.at[0, pl.ds(0, LANES)], res_s.at[d])
             took(wb.at[0, pl.ds(0, 16)], lef_s.at[d])
             took(cb.at[0], cor_s.at[d])
-            took(row, sc_s.at[d])
 
 
 def local(phase, incidence, triplet_weight, date_pairs):
     rows, pixel_count = phase.shape
     depth = -(-rows // 16) * 16
-    triplets, width = incidence.shape
-    me = lax.axis_index("ifg")
-    columns = lax.broadcasted_iota(jnp.int32, incidence.shape, 1)
-    columns = (columns + (columns // rows) * (depth - rows)).astype(jnp.float32)
-    plus = incidence == 1
-    first = jnp.min(jnp.where(plus, columns, 4096.0), axis=1)
-    second = jnp.max(jnp.where(plus, columns, -1.0), axis=1)
-    long = jnp.sum(jnp.where(incidence == -1, columns, 0.0), axis=1)
-    four = jnp.stack([first, second, long, triplet_weight])
-    lane = lax.broadcasted_iota(jnp.int32, (4, LANES), 1)
-    rest = jnp.where(lane // 16 == lax.rem(me, 8), jnp.tile(four[:, LANES:], (1, 8)), 0.0)
-    idx = jnp.pad(jnp.concatenate([four[:, :LANES], rest], axis=1), ((0, 4), (0, 0)))
-
+    triplets = incidence.shape[0]
     shares = pixel_count // LANES
     pairs = GROUP // 2 + 1
     vmem = pl.BlockSpec(memory_space=pltpu.VMEM)
+    pixes = lax.axis_size("pix")
     sems = [pltpu.SemaphoreType.DMA((GROUP,))] * 12
-    residual, correction, score = pl.pallas_call(
-        kernel,
+    residual, correction, relative = pl.pallas_call(
+        functools.partial(kernel, pixes * pixel_count),
         out_shape=(
             jax.ShapeDtypeStruct((triplets, pixel_count), jnp.bfloat16),
             jax.ShapeDtypeStruct((depth, pixel_count), jnp.bfloat16),
             jax.ShapeDtypeStruct((shares, 1, LANES), jnp.float32),
         ),
-        in_specs=[vmem] * 2,
+        in_specs=[vmem, pl.BlockSpec(memory_space=pl.ANY), vmem],
         out_specs=[vmem] * 3,
         scratch_shapes=[
+            pltpu.VMEM(incidence.shape, jnp.int32),
+            pltpu.VMEM((8, 2 * LANES), jnp.float32),
+            pltpu.VMEM((LANES, LANES), jnp.float32),
+            pltpu.VMEM((8, 2 * LANES), jnp.float32),
             pltpu.VMEM((depth, pixel_count), jnp.bfloat16),
             pltpu.VMEM((GROUP, depth, LANES), jnp.bfloat16),
             pltpu.VMEM((LANES, GROUP * depth), jnp.bfloat16),
@@ -239,18 +326,23 @@
             pltpu.VMEM((pairs, 2 * LANES, LANES), jnp.bfloat16),
             pltpu.VMEM((GROUP, depth, LANES), jnp.bfloat16),
             pltpu.VMEM((LANES, 2 * LANES), jnp.float32),
-            pltpu.VMEM((1, LANES), jnp.float32),
+            pltpu.VMEM((pixes, 1, LANES), jnp.float32),
+            pltpu.VMEM((2, LANES), jnp.float32),
+            pltpu.VMEM((GROUP, 2, LANES), jnp.float32),
+            pltpu.SemaphoreType.DMA,
             *sems,
+            pltpu.SemaphoreType.DMA((pixes,)),
+            pltpu.SemaphoreType.DMA((pixes,)),
+            pltpu.SemaphoreType.REGULAR,
+            pltpu.SemaphoreType.REGULAR,
+            pltpu.SemaphoreType.REGULAR,
         ],
         compiler_params=pltpu.CompilerParams(collective_id=0, has_side_effects=True),
-    )(phase, idx)
-
-    score = score.reshape(pixel_count)
-    all_pixels = pixel_count * lax.axis_size("pix")
-    relative = score / (lax.psum(jnp.sum(score), "pix") / all_pixels)
+    )(phase, incidence, triplet_weight.reshape(1, triplets))
+
     span = (date_pairs[:, 1] - date_pairs[:, 0]).astype(jnp.float32)
     corrected = phase.astype(jnp.float32) - correction[:rows].astype(jnp.float32) / (2.0 + span)[:, None]
-    return (residual.astype(jnp.float32), relative, corrected)
+    return (residual.astype(jnp.float32), relative.reshape(pixel_count), corrected)
 
 
 def solution(mesh):

time: 97.1 us -> 51.3 us (0.53)
  blocking collectives: 54.1 us -> 0 us
  Pallas kernels: 31.3 us -> 46.1 us
  other arithmetic: 7.08 us -> 3.62 us
  local copies, waits for them, and re-layouts: 2.7 us -> 0.69 us
    psum x1 -> x0, blocking collectives: 54.1 us -> none  [local(): relative = score / (lax.psum(jnp.sum(score), 'pix') / all_pixels)]
    pallas_call x1, Pallas kernels: 31.3 us -> 46.1 us  [local(): pl.pallas_call(functools.partial(kernel, pixes * pixel_count), out_shape=...]
    reduce_min x1 -> x0, other arithmetic: 1.43 us -> none  [local(): first = jnp.min(jnp.where(plus, columns, 4096.0), axis=1)]
    reduce_sum x1 -> x0, other arithmetic: 1.37 us -> none  [local(): relative = score / (lax.psum(jnp.sum(score), 'pix') / all_pixels)]
    unnamed x12 -> x8, local copies, waits for them, and re-layouts: 1.94 us -> 0.69 us
where the time goes in v2:
time: 51.3 us; the launch traced here: 51.1 us
  Pallas kernels  46.1 us (90%)
  other arithmetic  3.62 us (7%)
  local copies, waits for them, and re-layouts  0.69 us (1%)
  between operations  0.67 us (1%)
    pallas_call x1, Pallas kernels, local(): pl.pallas_call(functools.partial(kernel, pixes * pixel_count), out_shape=...  46.1 us
    convert_element_type x1, other arithmetic, local(): residual.astype(jnp.float32)  2.07 us

profile of v2, /device:TPU:1, one launch (start us, length us, event | category | flops | bytes accessed | tf_op | source)
XLA Modules:
  0.0 51.1 jit_solution(11882194958496257985)
XLA Ops:
  0.6 46.1 %shard_map.67 = (bf16[144,1536]{1,0:T(8,128)(2,1)}, bf16[80,1536]{1,0:T(8,128)(2,1)}, f32[12,1,128]{2,1,0:T(1,128)}) custom-call(bf16[75,1536]{1,0:T(8,128)(2,1)} %phase_ref.1, s32[144,1200]{1,0:T(8,128)} %inc_hbm.1, f32[1,144]{1,0:T(1,128)} %bitcast.5), custom_call_target="tpu_custom_call" | custom-call | tf_op jit(solution)/shard_map/pallas_call | solution.py:305
  46.7 0.0 copy-start
  46.8 0.0 copy-start.1
  46.8 2.1 %convert_element_type.13 = f32[144,1536]{1,0:T(8,128)} convert(bf16[144,1536]{1,0:T(8,128)(2,1)} %get-tuple-element.6) | non-fusion elementwise | flops 221184 | bytes 1327104 | tf_op jit(solution)/shard_map/convert_element_type | solution.py:345
  48.8 0.0 copy-start.3
  48.8 0.7 %copy-done.3 = s32[75,2]{0,1:T(2,128)S(1)} copy-done((s32[75,2]{0,1:T(2,128)S(1)}, s32[75,2]{0,1:T(2,128)}, u32[]{:S(2)}) %copy-start.3) | copy-done | bytes 624
  49.5 0.0 copy-done
  49.5 0.0 copy-done.1
  49.5 0.0 copy-start.2
  49.5 0.9 %divide_subtract_fusion = f32[75,1536]{1,0:T(8,128)} fusion(bf16[75,1536]{1,0:T(8,128)(2,1)S(1)} %copy-done, f32[75]{0:T(128)S(1)} %add_bitcast_fusion, bf16[80,1536]{1,0:T(8,128)(2,1)S(1)} %copy-done.1), kind=kLoop, calls=%fused_computation | loop fusion | flops 460800 | bytes 921900 | tf_op jit(solution)/shard_map/sub | solution.py:344
  50.5 0.0 copy-done.2
  50.5 0.6 %reduce = f32[12,128]{1,0:T(8,128)} reduce(f32[12,1,128]{2,1,0:T(1,128)S(1)} %copy-done.2, f32[]{:T(128)} %constant.4), dimensions={1}, to_apply=%get-tuple-element.7.reduce_sub_computation | reduce | bytes 12292 | tf_op jit(solution)/shard_map/pallas_call | solution.py:305
  (1 shorter events, 0.0 us)
Async XLA Ops:
  46.7 2.8 %copy-start = (bf16[75,1536]{1,0:T(8,128)(2,1)S(1)}, bf16[75,1536]{1,0:T(8,128)(2,1)}, u32[]{:S(2)}) copy-start(bf16[75,1536]{1,0:T(8,128)(2,1)} %phase_ref.1) | copy-start | bytes 691204
  46.8 2.8 %copy-start.1 = (bf16[80,1536]{1,0:T(8,128)(2,1)S(1)}, bf16[80,1536]{1,0:T(8,128)(2,1)}, u32[]{:S(2)}) copy-start(bf16[80,1536]{1,0:T(8,128)(2,1)} %get-tuple-element.8) | copy-start | bytes 737284
  48.8 0.7 %copy-start.3 = (s32[75,2]{0,1:T(2,128)S(1)}, s32[75,2]{0,1:T(2,128)}, u32[]{:S(2)}) copy-start(s32[75,2]{0,1:T(2,128)} %param.7) | copy-start | bytes 1804
  49.5 0.9 %copy-start.2 = (f32[12,1,128]{2,1,0:T(1,128)S(1)}, f32[12,1,128]{2,1,0:T(1,128)}, u32[]{:S(2)}) copy-start(f32[12,1,128]{2,1,0:T(1,128)} %get-tuple-element.7) | copy-start | bytes 18436

commit v3 on v2

v3 whole, which is shorter than its diff:
```python
import functools

import jax
import jax.numpy as jnp
from jax import lax
from jax.experimental import pallas as pl
from jax.experimental.pallas import tpu as pltpu
from jax.sharding import PartitionSpec as P

GROUP = 16
LANES = 128
VMEM = 16 * 1024 * 1024
INV_PI = 0.3183098861837907
PI_HI = 3.140625
PI_LO = 9.676535897932e-4
SIN = (-0.16666657096162138, 0.008333017284575896, -0.00019806614761156636, 2.6000538932920348e-06)
COS = (0.4999999954954239, -0.04166664072751474, 0.0013888403501702445, -2.476188593339371e-05, 2.607710003258223e-07)


def poly(coefs, z):
    out = jnp.full_like(z, coefs[-1])
    for c in coefs[-2::-1]:
        out = out * z + c
    return out


def sin_and_loss(x):
    k = jnp.floor(x * INV_PI + 0.5)
    r = (x - k * PI_HI) - k * PI_LO
    half = k * 0.5
    odd2 = (half - jnp.floor(half)) * 4.0
    sign = 1.0 - odd2
    z = r * r
    sine = sign * (r + (r * z) * poly(SIN, z))
    loss = odd2 + sign * (z * poly(COS, z))
    return sine, loss


def rank_of(device, core):
    return lax.rem(lax.rem(device, 4) - device // 4 - 2 * core + 7, 4)


def kernel(
    all_pixels,
    phase_hbm, inc_hbm, weight_hbm, dates_hbm, residual_ref, rel_ref, corrected_ref,
    inc, phase, weight, dates, res_ref, cor_ref, idx, rest16, wrow, padded, ph, pht, idxs, tiles, inct, iota, clo, wb, cb, acc, scores, fin_out, fin,
    in_sem, idx_s, idx_r, ph_s, ph_r, res_s, res_r, lef_s, lef_r, cor_s, cor_r, fin_s, fin_r, pix_s, pix_r,
    near1, near2, near4,
):
    me = lax.axis_index("ifg")
    pix = lax.axis_index("pix")
    x, y = me // 4, lax.rem(me, 4)
    core = lax.rem(pix, 2)
    rank = rank_of(me, core)
    active = rank < 3
    share = 3 * x + rank
    my_lanes = pl.ds(pl.multiple_of(share * LANES, LANES), LANES)
    rows = phase.shape[0]
    depth = padded.shape[0]
    pixes = scores.shape[0]
    steps = GROUP // 2 + 1

    def peer(j):
        return 4 * lax.rem(x + j // 4 + 2, 4) + lax.rem(y + lax.rem(j, 4) + 2, 4)

    def far(k):
        return lax.rem(pix + pixes // 2 + (k + 1) // 2 * (1 - 2 * lax.rem(k, 2)), pixes)

    barrier = pltpu.get_barrier_semaphore()

    def tell_group(k):
        pl.semaphore_signal(barrier, inc=1, device_id={"ifg": lax.rem(me + k, GROUP)}, device_id_type=pl.DeviceIdType.MESH)

    def tell_pix(sem, other):
        pl.semaphore_signal(sem, inc=1, device_id={"pix": lax.rem(other, pixes)}, device_id_type=pl.DeviceIdType.MESH)

    def tell_along_z(sem, distance):
        tell_pix(sem, pix + 2 * distance)
        tell_pix(sem, pix + pixes - 2 * distance)

    read_inc = pltpu.make_async_copy(inc_hbm, inc, in_sem.at[0])
    read_inc.start()
    read_phase = pltpu.make_async_copy(phase_hbm, phase, in_sem.at[1])
    read_phase.start()
    read_weight = pltpu.make_async_copy(weight_hbm, weight, in_sem.at[2])
    read_weight.start()
    read_dates = pltpu.make_async_copy(dates_hbm, dates, in_sem.at[3])
    read_dates.start()
    pl.loop(1, GROUP)(tell_group)
    across = 2 * (pix // 2) + 1 - core
    tell_pix(barrier, across)
    tell_along_z(barrier, 1)
    tell_pix(barrier, across + 2)
    tell_pix(barrier, across + pixes - 2)

    iota[...] = lax.broadcasted_iota(jnp.int32, iota.shape, 0).astype(jnp.float32).astype(jnp.bfloat16)
    acc[...] = jnp.zeros_like(acc)
    scores[pix] = jnp.zeros(scores.shape[1:], scores.dtype)
    wrow[...] = jnp.zeros_like(wrow)
    rest16[...] = jnp.zeros_like(rest16)
    padded[...] = jnp.zeros_like(padded)

    read_inc.wait()
    read_phase.wait()
    read_weight.wait()
    read_dates.wait()
    padded[0:rows, :] = phase[...]
    wrow[0:1, 0 : weight.shape[1]] = weight[...]
    width = inc.shape[1]
    column = lax.broadcasted_iota(jnp.int32, (1, width), 1).astype(jnp.float32)
    column = column + jnp.floor((column + 0.5) * (1.0 / rows)) * (depth - rows)
    value = inc[...]
    plus = value == 1
    first = jnp.min(jnp.where(plus, column, 4096.0), axis=1, keepdims=True)
    second = jnp.max(jnp.where(plus, column, -1.0), axis=1, keepdims=True)
    long = jnp.sum(jnp.where(value == -1, column, 0.0), axis=1, keepdims=True)
    lane = lax.broadcasted_iota(jnp.int32, (inc.shape[0], LANES), 1)
    three = jnp.where(lane == 0, first, jnp.where(lane == 1, second, long))
    spot = 16 * lax.rem(me, 8)
    rest16[pl.ds(pl.multiple_of(spot, 16), 16), :] = three[LANES:]
    line = lax.broadcasted_iota(jnp.int32, (8, LANES), 0)
    for q, t, w in (
        (0, three[:LANES], wrow[:, :LANES]),
        (1, rest16[...], pltpu.roll(wrow[:, LANES:], spot, 1)),
    ):
        t = jnp.where(line < 3, jnp.transpose(t)[0:8], 0.0)
        idx[:, q * LANES : (q + 1) * LANES] = jnp.where(line == 3, jnp.broadcast_to(w[0:1], t.shape), t)

    pl.semaphore_wait(barrier, GROUP + 4)
    tell_along_z(near1, 1)

    def put(src, dst, send, recv, device):
        @pl.when(device != me)
        def _():
            pltpu.make_async_remote_copy(
                src_ref=src, dst_ref=dst, send_sem=send, recv_sem=recv,
                device_id={"ifg": device}, device_id_type=pl.DeviceIdType.MESH,
            ).start()

        @pl.when(device == me)
        def _():
            pltpu.make_async_copy(src, dst, recv).start()

    def took(ref, sem):
        pltpu.make_async_copy(ref, ref, sem).wait()

    def to_shares(body):
        @pl.loop(0, GROUP)
        def _(j):
            device = peer(j)
            their = rank_of(device, core)

            @pl.when(their < 3)
            def _():
                body(device, pl.multiple_of((3 * (device // 4) + their) * LANES, LANES))

    to_shares(lambda d, at: put(idx, idxs.at[me], idx_s.at[d], idx_r.at[me], d))
    to_shares(lambda d, at: put(padded.at[:, pl.ds(at, LANES)], ph.at[me], ph_s.at[d], ph_r.at[me], d))

    pl.semaphore_wait(near1, 2)
    tell_along_z(near2, 2)
    pl.semaphore_wait(near2, 2)
    tell_along_z(near4, 4)

    def pair(j):
        return lax.rem(me // 2 + j, GROUP // 2)

    def build(j):
        t = tiles[j]
        at = iota[...]
        one = jnp.ones(at.shape, jnp.bfloat16)
        for b in range(GROUP):
            rel = (t - float(b * depth)).astype(jnp.bfloat16)
            both = jnp.logical_or(at == rel[0:1], at == rel[1:2])
            signed = jnp.where(at == rel[2:3], -one, jnp.where(both, one, jnp.zeros_like(one)))
            inct[j, b * depth : (b + 1) * depth, :] = signed

    def finish(j):
        sine, loss = sin_and_loss(clo[...])
        acc[...] += loss * tiles[j, 3:4, :]
        wb[j] = jnp.transpose(sine).astype(jnp.bfloat16)

    def send_rows(j):
        if j < GROUP // 2:
            for q in range(2):
                d = 2 * pair(j) + q
                put(wb.at[j, pl.ds(q * LANES, LANES)], res_ref.at[pl.ds(0, LANES), my_lanes], res_s.at[d], res_r.at[share], d)
            return

        @pl.loop(0, GROUP)
        def _(k):
            d = peer(k)
            put(
                wb.at[j, pl.ds(pl.multiple_of(16 * d, 16), 16)],
                res_ref.at[pl.ds(LANES, 16), my_lanes], lef_s.at[d], lef_r.at[share], d,
            )

    @pl.when(active)
    def _():
        @pl.loop(0, GROUP)
        def _(d):
            took(idxs.at[d], idx_r.at[d])

        for j in range(GROUP // 2):
            for q in range(2):
                tiles[j, :, q * LANES : (q + 1) * LANES] = idxs[2 * pair(j) + q, :, 0:LANES]
        for q in range(2):
            rest = idxs[8 * q, :, LANES:]
            for i in range(1, 8):
                rest = rest + idxs[8 * q + i, :, LANES:]
            tiles[GROUP // 2, :, q * LANES : (q + 1) * LANES] = rest
        build(0)

        for half in range(2):
            for d in range(8 * half, 8 * half + 8):
                took(ph.at[d], ph_r.at[d])
            block = ph[8 * half : 8 * half + 8].reshape(8 * depth, LANES)
            pht[:, 8 * depth * half : 8 * depth * (half + 1)] = jnp.transpose(block.astype(jnp.float32)).astype(jnp.bfloat16)

        for j in range(steps):
            closure = jnp.dot(pht[...], inct[j], preferred_element_type=jnp.float32)
            if j > 0:
                finish(j - 1)
            if j + 1 < steps:
                build(j + 1)
            clo[...] = closure
            if j > 0:
                send_rows(j - 1)
        finish(steps - 1)

        total = tiles[0, 3:4, :]
        for j in range(1, steps):
            total = total + tiles[j, 3:4, :]
        both = acc[:, 0:LANES] + acc[:, LANES:]
        misfit = jnp.sum(jnp.transpose(both), axis=0, keepdims=True)
        scores[pix] = misfit / jnp.sum(total, axis=1, keepdims=True)

    pl.semaphore_wait(near4, 2)

    @pl.loop(0, pixes - 1)
    def _(k):
        other = far(k)
        pltpu.make_async_remote_copy(
            src_ref=scores.at[pix], dst_ref=scores.at[pix], send_sem=pix_s.at[other], recv_sem=pix_r.at[pix],
            device_id={"pix": other}, device_id_type=pl.DeviceIdType.MESH,
        ).start()

    @pl.when(active)
    def _():
        send_rows(steps - 1)

        @pl.loop(0, 4)
        def _(j):
            c = lax.rem(x + 2 + j, 4)
            at = pl.ds(pl.multiple_of(c * 4 * depth, 4 * depth), 4 * depth)
            corr = jnp.zeros((4 * depth, LANES), jnp.float32)
            for p in range(steps):
                corr = corr + jnp.dot(inct[p, at, :], wb[p], preferred_element_type=jnp.float32)
            cb[pl.ds(4 * c, 4)] = corr.astype(jnp.bfloat16).reshape(4, depth, LANES)
            for q in range(4):
                d = 4 * c + q
                put(cb.at[d], cor_ref.at[:, my_lanes], cor_s.at[d], cor_r.at[share], d)

    @pl.loop(0, pixes - 1)
    def _(k):
        other = far(k)
        took(scores.at[other], pix_r.at[other])

    fin_out[0:1] = scores[pix]
    fin_out[1:2] = jnp.sum(scores[...], axis=0)
    slot = jnp.where(active, share, 12 + x)

    @pl.loop(0, GROUP)
    def _(k):
        d = peer(k)
        put(fin_out, fin.at[slot], fin_s.at[d], fin_r.at[slot], d)

    @pl.loop(0, pixes - 1)
    def _(k):
        took(scores.at[pix], pix_s.at[far(k)])

    @pl.loop(1, GROUP)
    def _(k):
        d = lax.rem(me + k, GROUP)

        @pl.when(rank_of(d, core) < 3)
        def _():
            took(idxs.at[0], idx_s.at[d])
            took(ph.at[0], ph_s.at[d])

        @pl.when(active)
        def _():
            took(wb.at[0, pl.ds(0, LANES)], res_s.at[d])
            took(wb.at[0, pl.ds(0, 16)], lef_s.at[d])
            took(cb.at[0], cor_s.at[d])

    @pl.loop(0, 12)
    def _(s):
        lanes = pl.ds(pl.multiple_of(s * LANES, LANES), LANES)
        took(res_ref.at[pl.ds(0, LANES), lanes], res_r.at[s])
        took(res_ref.at[pl.ds(LANES, 16), lanes], lef_r.at[s])
        took(cor_ref.at[:, lanes], cor_r.at[s])

    span = (dates[1:2] - dates[0:1]).astype(jnp.float32)
    damp = jnp.concatenate([1.0 / (2.0 + span), jnp.zeros((1, LANES - rows), jnp.float32)], axis=1)
    damp = jnp.transpose(jnp.broadcast_to(damp, (LANES, LANES)))[:rows]

    @pl.loop(0, 12)
    def _(s):
        lanes = pl.ds(pl.multiple_of(s * LANES, LANES), LANES)
        residual_ref[:, lanes] = res_ref[:, lanes].astype(jnp.float32)
        corrected_ref[:, lanes] = phase[:, lanes].astype(jnp.float32) - cor_ref[0:rows, lanes].astype(jnp.float32) * damp

    @pl.loop(1, GROUP)
    def _(k):
        took(fin_out, fin_s.at[lax.rem(me + k, GROUP)])

    @pl.loop(0, GROUP)
    def _(s):
        took(fin.at[s], fin_r.at[s])

    everything = jnp.sum(jnp.sum(fin[...], axis=0)[1:2], axis=1, keepdims=True)
    for s in range(12):
        rel_ref[:, s * LANES : (s + 1) * LANES] = fin[s, 0:1] / (everything / all_pixels)


def local(phase, incidence, triplet_weight, date_pairs):
    rows, pixel_count = phase.shape
    depth = -(-rows // 16) * 16
    triplets = incidence.shape[0]
    pairs = GROUP // 2 + 1
    hbm = pl.BlockSpec(memory_space=pltpu.HBM)
    vmem = pl.BlockSpec(memory_space=pltpu.VMEM)
    pixes = lax.axis_size("pix")
    sems = [pltpu.SemaphoreType.DMA((GROUP,))] * 12
    operands = (phase, incidence, triplet_weight.reshape(1, triplets), date_pairs.T)
    operands = [pltpu.with_memory_space_constraint(a, pltpu.HBM) for a in operands]
    residual, relative, corrected = pl.pallas_call(
        functools.partial(kernel, pixes * pixel_count),
        out_shape=(
            jax.ShapeDtypeStruct((triplets, pixel_count), jnp.float32),
            jax.ShapeDtypeStruct((1, pixel_count), jnp.float32),
            jax.ShapeDtypeStruct((rows, pixel_count), jnp.float32),
        ),
        in_specs=[hbm] * 4,
        out_specs=[vmem] * 3,
        scratch_shapes=[
            pltpu.VMEM(incidence.shape, jnp.int32),
            pltpu.VMEM(phase.shape, jnp.bfloat16),
            pltpu.VMEM((1, triplets), jnp.float32),
            pltpu.VMEM((2, rows), jnp.int32),
            pltpu.VMEM((triplets, pixel_count), jnp.bfloat16),
            pltpu.VMEM((depth, pixel_count), jnp.bfloat16),
            pltpu.VMEM((8, 2 * LANES), jnp.float32),
            pltpu.VMEM((LANES, LANES), jnp.float32),
            pltpu.VMEM((8, 2 * LANES), jnp.float32),
            pltpu.VMEM((depth, pixel_count), jnp.bfloat16),
            pltpu.VMEM((GROUP, depth, LANES), jnp.bfloat16),
            pltpu.VMEM((LANES, GROUP * depth), jnp.bfloat16),
            pltpu.VMEM((GROUP, 8, 2 * LANES), jnp.float32),
            pltpu.VMEM((pairs, 8, 2 * LANES), jnp.float32),
            pltpu.VMEM((pairs, GROUP * depth, 2 * LANES), jnp.bfloat16),
            pltpu.VMEM((depth, 2 * LANES), jnp.bfloat16),
            pltpu.VMEM((LANES, 2 * LANES), jnp.float32),
            pltpu.VMEM((pairs, 2 * LANES, LANES), jnp.bfloat16),
            pltpu.VMEM((GROUP, depth, LANES), jnp.bfloat16),
            pltpu.VMEM((LANES, 2 * LANES), jnp.float32),
            pltpu.VMEM((pixes, 1, LANES), jnp.float32),
            pltpu.VMEM((2, LANES), jnp.float32),
            pltpu.VMEM((GROUP, 2, LANES), jnp.float32),
            pltpu.SemaphoreType.DMA((4,)),
            *sems,
            pltpu.SemaphoreType.DMA((pixes,)),
            pltpu.SemaphoreType.DMA((pixes,)),
            pltpu.SemaphoreType.REGULAR,
            pltpu.SemaphoreType.REGULAR,
            pltpu.SemaphoreType.REGULAR,
        ],
        compiler_params=pltpu.CompilerParams(collective_id=0, has_side_effects=True, vmem_limit_bytes=VMEM),
    )(*operands)
    return (residual, relative.reshape(pixel_count), corrected)


def solution(mesh):
    return jax.shard_map(
        local,
        mesh=mesh,
        in_specs=(P("ifg", "pix"), P("ifg", None), P("ifg"), P("ifg", None)),
        out_specs=(P("ifg", "pix"), P("pix"), P("ifg", "pix")),
        check_vma=False,
    )
```

time: 51.3 us -> 43.8 us (0.85)
  Pallas kernels: 46.1 us -> 40.7 us
  other arithmetic: 3.62 us -> 0.62 us
  local copies, waits for them, and re-layouts: 0.69 us -> 1.69 us
    pallas_call x1, Pallas kernels: 46.1 us -> 40.7 us  [local(): pl.pallas_call(functools.partial(kernel, pixes * pixel_count), out_shape=...]
    convert_element_type x1 -> x0, other arithmetic: 2.07 us -> none  [local(): residual.astype(jnp.float32)]
    unnamed x8 -> x2, local copies, waits for them, and re-layouts: 0.69 us -> 1.69 us
    sub x1 -> x0, other arithmetic: 0.92 us -> none  [local(): phase.astype(jnp.float32)]
where the time goes in v3:
time: 43.8 us; the launch traced here: 43.7 us
  Pallas kernels  40.7 us (93%)
  local copies, waits for them, and re-layouts  1.69 us (4%)
  between operations  0.64 us (1%)
  other arithmetic  0.62 us (1%)
    pallas_call x1, Pallas kernels, local(): pl.pallas_call(functools.partial(kernel, pixes * pixel_count), out_shape=...  40.7 us
    unnamed x2, local copies, waits for them, and re-layouts  1.69 us

profile of v3, /device:TPU:1, one launch (start us, length us, event | category | flops | bytes accessed | tf_op | source)
XLA Modules:
  0.0 43.7 jit_solution(6487757374749522085)
XLA Ops:
  0.6 40.7 %shard_map.67 = (f32[144,1536]{1,0:T(8,128)S(1)}, f32[1,1536]{1,0:T(1,128)S(1)}, f32[75,1536]{1,0:T(8,128)S(1)}) custom-call(bf16[75,1536]{1,0:T(8,128)(2,1)} %phase_hbm.1, s32[144,1200]{1,0:T(8,128)} %inc_hbm.1, f32[1,144]{1,0:T(1,128)} %bitcast.2, s32[2,75]{1,0:T(2,128)} %bitcast.3), custom_call_target="tpu_custom_call" | custom-call | tf_op jit(solution)/shard_map/pallas_call | solution.py:338
  41.4 0.6 %reduce = f32[1536]{0:T(1024)} reduce(f32[1,1536]{1,0:T(1,128)S(1)} %get-tuple-element.7, f32[]{:T(128)} %constant.2), dimensions={0}, to_apply=%get-tuple-element.7.reduce_sub_computation | reduce | bytes 12292 | tf_op jit(solution)/shard_map/pallas_call | solution.py:338
  42.0 0.9 %copy.9 = f32[144,1536]{1,0:T(8,128)} copy(f32[144,1536]{1,0:T(8,128)S(1)} %get-tuple-element.12) | data formatting | bytes 1769472
  42.9 0.8 %copy.10 = f32[75,1536]{1,0:T(8,128)} copy(f32[75,1536]{1,0:T(8,128)S(1)} %get-tuple-element.14) | data formatting | bytes 921600

commit v4 on v3

--- a/solution.py
+++ b/solution.py
@@ -10,30 +10,27 @@
 GROUP = 16
 LANES = 128
 VMEM = 16 * 1024 * 1024
-INV_PI = 0.3183098861837907
-PI_HI = 3.140625
-PI_LO = 9.676535897932e-4
-SIN = (-0.16666657096162138, 0.008333017284575896, -0.00019806614761156636, 2.6000538932920348e-06)
-COS = (0.4999999954954239, -0.04166664072751474, 0.0013888403501702445, -2.476188593339371e-05, 2.607710003258223e-07)
+INV_2PI = 0.15915494309189535
+TWO_PI_HI = 6.28125
+TWO_PI_LO = 1.9353071795864769e-3
+SIN = (-0.041666642741103474, 0.000520813580633296, -3.094783609930149e-06, 1.0156463124188801e-08)
+COS = (-0.12499999887388552, 0.0026041650454957602, -2.170063047895746e-05, 9.672611781418933e-08, -2.5465921654786513e-10)
 
 
 def poly(coefs, z):
-    out = jnp.full_like(z, coefs[-1])
-    for c in coefs[-2::-1]:
+    out = z * coefs[-1] + coefs[-2]
+    for c in coefs[-3::-1]:
         out = out * z + c
     return out
 
 
-def sin_and_loss(x):
-    k = jnp.floor(x * INV_PI + 0.5)
-    r = (x - k * PI_HI) - k * PI_LO
-    half = k * 0.5
-    odd2 = (half - jnp.floor(half)) * 4.0
-    sign = 1.0 - odd2
+def sin_and_twice_loss(x):
+    k = jnp.round(x * INV_2PI)
+    r = (x - k * TWO_PI_HI) - k * TWO_PI_LO
     z = r * r
-    sine = sign * (r + (r * z) * poly(SIN, z))
-    loss = odd2 + sign * (z * poly(COS, z))
-    return sine, loss
+    sine = r + (r * z) * poly(SIN, z)
+    cosine = 1.0 + z * poly(COS, z)
+    return sine * cosine, sine * sine
 
 
 def rank_of(device, core):
@@ -44,7 +41,7 @@
     all_pixels,
     phase_hbm, inc_hbm, weight_hbm, dates_hbm, residual_ref, rel_ref, corrected_ref,
     inc, phase, weight, dates, res_ref, cor_ref, idx, rest16, wrow, padded, ph, pht, idxs, tiles, inct, iota, clo, wb, cb, acc, scores, fin_out, fin,
-    in_sem, idx_s, idx_r, ph_s, ph_r, res_s, res_r, lef_s, lef_r, cor_s, cor_r, fin_s, fin_r, pix_s, pix_r,
+    in_sem, ph_r, idx_s, idx_r, ph_s, res_s, res_r, lef_s, cor_s, cor_r, fin_s, fin_r, pix_s, pix_r,
     near1, near2, near4,
 ):
     me = lax.axis_index("ifg")
@@ -108,7 +105,6 @@
     wrow[0:1, 0 : weight.shape[1]] = weight[...]
     width = inc.shape[1]
     column = lax.broadcasted_iota(jnp.int32, (1, width), 1).astype(jnp.float32)
-    column = column + jnp.floor((column + 0.5) * (1.0 / rows)) * (depth - rows)
     value = inc[...]
     plus = value == 1
     first = jnp.min(jnp.where(plus, column, 4096.0), axis=1, keepdims=True)
@@ -118,13 +114,15 @@
     three = jnp.where(lane == 0, first, jnp.where(lane == 1, second, long))
     spot = 16 * lax.rem(me, 8)
     rest16[pl.ds(pl.multiple_of(spot, 16), 16), :] = three[LANES:]
-    line = lax.broadcasted_iota(jnp.int32, (8, LANES), 0)
+    here = lax.broadcasted_iota(jnp.int32, (8, LANES), 1) // 16 == lax.rem(me, 8)
     for q, t, w in (
         (0, three[:LANES], wrow[:, :LANES]),
         (1, rest16[...], pltpu.roll(wrow[:, LANES:], spot, 1)),
     ):
-        t = jnp.where(line < 3, jnp.transpose(t)[0:8], 0.0)
-        idx[:, q * LANES : (q + 1) * LANES] = jnp.where(line == 3, jnp.broadcast_to(w[0:1], t.shape), t)
+        t = jnp.transpose(t)[0:8]
+        block = jnp.floor((t + 0.5) * (1.0 / rows))
+        message = jnp.concatenate([(t - block * rows)[0:3], block[0:3], w[0:1], jnp.zeros_like(w[0:1])], axis=0)
+        idx[:, q * LANES : (q + 1) * LANES] = jnp.where(jnp.logical_or(q == 0, here), message, 0.0)
 
     pl.semaphore_wait(barrier, GROUP + 4)
     tell_along_z(near1, 1)
@@ -154,8 +152,8 @@
             def _():
                 body(device, pl.multiple_of((3 * (device // 4) + their) * LANES, LANES))
 
-    to_shares(lambda d, at: put(idx, idxs.at[me], idx_s.at[d], idx_r.at[me], d))
-    to_shares(lambda d, at: put(padded.at[:, pl.ds(at, LANES)], ph.at[me], ph_s.at[d], ph_r.at[me], d))
+    to_shares(lambda d, at: put(idx, idxs.at[me], idx_s, idx_r, d))
+    to_shares(lambda d, at: put(padded.at[:, pl.ds(at, LANES)], ph.at[me], ph_s, ph_r.at[me // 8], d))
 
     pl.semaphore_wait(near1, 2)
     tell_along_z(near2, 2)
@@ -168,23 +166,29 @@
     def build(j):
         t = tiles[j]
         at = iota[...]
-        one = jnp.ones(at.shape, jnp.bfloat16)
+        lines = []
+        blocks = []
+        for i in range(3):
+            row = jnp.broadcast_to(t[i : i + 1], at.shape).astype(jnp.bfloat16)
+            lines.append(jnp.where(at == row, jnp.full_like(at, -1.0 if i == 2 else 1.0), jnp.zeros_like(at)))
+            blocks.append(jnp.broadcast_to(t[3 + i : 4 + i], (16, at.shape[1])).astype(jnp.bfloat16))
+        one = jnp.ones_like(blocks[0])
         for b in range(GROUP):
-            rel = (t - float(b * depth)).astype(jnp.bfloat16)
-            both = jnp.logical_or(at == rel[0:1], at == rel[1:2])
-            signed = jnp.where(at == rel[2:3], -one, jnp.where(both, one, jnp.zeros_like(one)))
-            inct[j, b * depth : (b + 1) * depth, :] = signed
+            inside = [jnp.where(v == one * b, one, jnp.zeros_like(one)) for v in blocks]
+            for g in range(depth // 16):
+                terms = [v * line[16 * g : 16 * g + 16] for v, line in zip(inside, lines)]
+                inct[j, b * depth + 16 * g : b * depth + 16 * g + 16, :] = terms[0] + terms[1] + terms[2]
 
     def finish(j):
-        sine, loss = sin_and_loss(clo[...])
-        acc[...] += loss * tiles[j, 3:4, :]
+        sine, loss = sin_and_twice_loss(clo[...])
+        acc[...] += loss * (0.5 * tiles[j, 6:7, :])
         wb[j] = jnp.transpose(sine).astype(jnp.bfloat16)
 
     def send_rows(j):
         if j < GROUP // 2:
             for q in range(2):
                 d = 2 * pair(j) + q
-                put(wb.at[j, pl.ds(q * LANES, LANES)], res_ref.at[pl.ds(0, LANES), my_lanes], res_s.at[d], res_r.at[share], d)
+                put(wb.at[j, pl.ds(q * LANES, LANES)], res_ref.at[pl.ds(0, LANES), my_lanes], res_s, res_r, d)
             return
 
         @pl.loop(0, GROUP)
@@ -192,14 +196,12 @@
             d = peer(k)
             put(
                 wb.at[j, pl.ds(pl.multiple_of(16 * d, 16), 16)],
-                res_ref.at[pl.ds(LANES, 16), my_lanes], lef_s.at[d], lef_r.at[share], d,
+                res_ref.at[pl.ds(LANES, 16), my_lanes], lef_s, res_r, d,
             )
 
     @pl.when(active)
     def _():
-        @pl.loop(0, GROUP)
-        def _(d):
-            took(idxs.at[d], idx_r.at[d])
+        took(idxs, idx_r)
 
         for j in range(GROUP // 2):
             for q in range(2):
@@ -212,8 +214,7 @@
         build(0)
 
         for half in range(2):
-            for d in range(8 * half, 8 * half + 8):
-                took(ph.at[d], ph_r.at[d])
+            took(ph.at[pl.ds(8 * half, 8)], ph_r.at[half])
             block = ph[8 * half : 8 * half + 8].reshape(8 * depth, LANES)
             pht[:, 8 * depth * half : 8 * depth * (half + 1)] = jnp.transpose(block.astype(jnp.float32)).astype(jnp.bfloat16)
 
@@ -228,9 +229,9 @@
                 send_rows(j - 1)
         finish(steps - 1)
 
-        total = tiles[0, 3:4, :]
+        total = tiles[0, 6:7, :]
         for j in range(1, steps):
-            total = total + tiles[j, 3:4, :]
+            total = total + tiles[j, 6:7, :]
         both = acc[:, 0:LANES] + acc[:, LANES:]
         misfit = jnp.sum(jnp.transpose(both), axis=0, keepdims=True)
         scores[pix] = misfit / jnp.sum(total, axis=1, keepdims=True)
@@ -241,7 +242,7 @@
     def _(k):
         other = far(k)
         pltpu.make_async_remote_copy(
-            src_ref=scores.at[pix], dst_ref=scores.at[pix], send_sem=pix_s.at[other], recv_sem=pix_r.at[pix],
+            src_ref=scores.at[pix], dst_ref=scores.at[pix], send_sem=pix_s, recv_sem=pix_r,
             device_id={"pix": other}, device_id_type=pl.DeviceIdType.MESH,
         ).start()
 
@@ -259,12 +260,9 @@
             cb[pl.ds(4 * c, 4)] = corr.astype(jnp.bfloat16).reshape(4, depth, LANES)
             for q in range(4):
                 d = 4 * c + q
-                put(cb.at[d], cor_ref.at[:, my_lanes], cor_s.at[d], cor_r.at[share], d)
-
-    @pl.loop(0, pixes - 1)
-    def _(k):
-        other = far(k)
-        took(scores.at[other], pix_r.at[other])
+                put(cb.at[d], cor_ref.at[:, my_lanes], cor_s, cor_r, d)
+
+    took(scores.at[pl.ds(0, pixes - 1)], pix_r)
 
     fin_out[0:1] = scores[pix]
     fin_out[1:2] = jnp.sum(scores[...], axis=0)
@@ -273,33 +271,26 @@
     @pl.loop(0, GROUP)
     def _(k):
         d = peer(k)
-        put(fin_out, fin.at[slot], fin_s.at[d], fin_r.at[slot], d)
-
-    @pl.loop(0, pixes - 1)
-    def _(k):
-        took(scores.at[pix], pix_s.at[far(k)])
-
-    @pl.loop(1, GROUP)
-    def _(k):
-        d = lax.rem(me + k, GROUP)
-
-        @pl.when(rank_of(d, core) < 3)
-        def _():
-            took(idxs.at[0], idx_s.at[d])
-            took(ph.at[0], ph_s.at[d])
-
-        @pl.when(active)
-        def _():
-            took(wb.at[0, pl.ds(0, LANES)], res_s.at[d])
-            took(wb.at[0, pl.ds(0, 16)], lef_s.at[d])
-            took(cb.at[0], cor_s.at[d])
-
-    @pl.loop(0, 12)
-    def _(s):
-        lanes = pl.ds(pl.multiple_of(s * LANES, LANES), LANES)
-        took(res_ref.at[pl.ds(0, LANES), lanes], res_r.at[s])
-        took(res_ref.at[pl.ds(LANES, 16), lanes], lef_r.at[s])
-        took(cor_ref.at[:, lanes], cor_r.at[s])
+        put(fin_out, fin.at[slot], fin_s, fin_r, d)
+
+    others = GROUP - 1
+    took(scores.at[pl.ds(0, pixes - 1)], pix_s)
+
+    @pl.when(active)
+    def _():
+        took(idxs.at[pl.ds(0, 11)], idx_s)
+        took(ph.at[pl.ds(0, 11)], ph_s)
+        took(inct.at[0, pl.ds(0, others * LANES // 2)], res_s)
+        took(wb.at[0, pl.ds(0, others * 16)], lef_s)
+        took(cb.at[pl.ds(0, others)], cor_s)
+
+    @pl.when(rank == 3)
+    def _():
+        took(idxs.at[pl.ds(0, 12)], idx_s)
+        took(ph.at[pl.ds(0, 12)], ph_s)
+
+    took(res_ref, res_r)
+    took(cor_ref, cor_r)
 
     span = (dates[1:2] - dates[0:1]).astype(jnp.float32)
     damp = jnp.concatenate([1.0 / (2.0 + span), jnp.zeros((1, LANES - rows), jnp.float32)], axis=1)
@@ -311,13 +302,8 @@
         residual_ref[:, lanes] = res_ref[:, lanes].astype(jnp.float32)
         corrected_ref[:, lanes] = phase[:, lanes].astype(jnp.float32) - cor_ref[0:rows, lanes].astype(jnp.float32) * damp
 
-    @pl.loop(1, GROUP)
-    def _(k):
-        took(fin_out, fin_s.at[lax.rem(me + k, GROUP)])
-
-    @pl.loop(0, GROUP)
-    def _(s):
-        took(fin.at[s], fin_r.at[s])
+    took(fin.at[pl.ds(0, others)], fin_s)
+    took(fin, fin_r)
 
     everything = jnp.sum(jnp.sum(fin[...], axis=0)[1:2], axis=1, keepdims=True)
     for s in range(12):
@@ -332,7 +318,6 @@
     hbm = pl.BlockSpec(memory_space=pltpu.HBM)
     vmem = pl.BlockSpec(memory_space=pltpu.VMEM)
     pixes = lax.axis_size("pix")
-    sems = [pltpu.SemaphoreType.DMA((GROUP,))] * 12
     operands = (phase, incidence, triplet_weight.reshape(1, triplets), date_pairs.T)
     operands = [pltpu.with_memory_space_constraint(a, pltpu.HBM) for a in operands]
     residual, relative, corrected = pl.pallas_call(
@@ -369,12 +354,9 @@
             pltpu.VMEM((2, LANES), jnp.float32),
             pltpu.VMEM((GROUP, 2, LANES), jnp.float32),
             pltpu.SemaphoreType.DMA((4,)),
-            *sems,
-            pltpu.SemaphoreType.DMA((pixes,)),
-            pltpu.SemaphoreType.DMA((pixes,)),
-            pltpu.SemaphoreType.REGULAR,
-            pltpu.SemaphoreType.REGULAR,
-            pltpu.SemaphoreType.REGULAR,
+            pltpu.SemaphoreType.DMA((2,)),
+            *[pltpu.SemaphoreType.DMA] * 12,
+            *[pltpu.SemaphoreType.REGULAR] * 3,
         ],
         compiler_params=pltpu.CompilerParams(collective_id=0, has_side_effects=True, vmem_limit_bytes=VMEM),
     )(*operands)

time: 43.8 us -> 40.6 us (0.927)
  Pallas kernels: 40.7 us -> 37.5 us
    pallas_call x1, Pallas kernels: 40.7 us -> 37.5 us  [local(): pl.pallas_call(functools.partial(kernel, pixes * pixel_count), out_shape=...]
where the time goes in v4:
time: 40.6 us; the launch traced here: 40.5 us
  Pallas kernels  37.5 us (92%)
  local copies, waits for them, and re-layouts  1.69 us (4%)
  between operations  0.64 us (2%)
  other arithmetic  0.62 us (2%)
    pallas_call x1, Pallas kernels, local(): pl.pallas_call(functools.partial(kernel, pixes * pixel_count), out_shape=...  37.5 us
    unnamed x2, local copies, waits for them, and re-layouts  1.69 us

profile of v4, /device:TPU:1, one launch (start us, length us, event | category | flops | bytes accessed | tf_op | source)
XLA Modules:
  0.0 40.5 jit_solution(5982716742219852013)
XLA Ops:
  0.6 37.5 %shard_map.67 = (f32[144,1536]{1,0:T(8,128)S(1)}, f32[1,1536]{1,0:T(1,128)S(1)}, f32[75,1536]{1,0:T(8,128)S(1)}) custom-call(bf16[75,1536]{1,0:T(8,128)(2,1)} %phase_hbm.1, s32[144,1200]{1,0:T(8,128)} %inc_hbm.1, f32[1,144]{1,0:T(1,128)} %bitcast.2, s32[2,75]{1,0:T(2,128)} %bitcast.3), custom_call_target="tpu_custom_call" | custom-call | tf_op jit(solution)/shard_map/pallas_call | solution.py:323
  38.2 0.6 %reduce = f32[1536]{0:T(1024)} reduce(f32[1,1536]{1,0:T(1,128)S(1)} %get-tuple-element.7, f32[]{:T(128)} %constant.2), dimensions={0}, to_apply=%get-tuple-element.7.reduce_sub_computation | reduce | bytes 12292 | tf_op jit(solution)/shard_map/pallas_call | solution.py:323
  38.8 0.9 %copy.9 = f32[144,1536]{1,0:T(8,128)} copy(f32[144,1536]{1,0:T(8,128)S(1)} %get-tuple-element.12) | data formatting | bytes 1769472
  39.7 0.8 %copy.10 = f32[75,1536]{1,0:T(8,128)} copy(f32[75,1536]{1,0:T(8,128)S(1)} %get-tuple-element.14) | data formatting | bytes 921600

commit v5 on v4

--- a/solution.py
+++ b/solution.py
@@ -121,8 +121,9 @@
     ):
         t = jnp.transpose(t)[0:8]
         block = jnp.floor((t + 0.5) * (1.0 / rows))
-        message = jnp.concatenate([(t - block * rows)[0:3], block[0:3], w[0:1], jnp.zeros_like(w[0:1])], axis=0)
-        idx[:, q * LANES : (q + 1) * LANES] = jnp.where(jnp.logical_or(q == 0, here), message, 0.0)
+        high = w[0:1].astype(jnp.bfloat16).astype(jnp.float32)
+        message = jnp.concatenate([(t - block * rows)[0:3], block[0:3], high, w[0:1] - high], axis=0)
+        idx[:, q * LANES : (q + 1) * LANES] = jnp.where(jnp.logical_or(q == 0, here), message, 0.0).astype(jnp.bfloat16)
 
     pl.semaphore_wait(barrier, GROUP + 4)
     tell_along_z(near1, 1)
@@ -179,25 +180,18 @@
                 terms = [v * line[16 * g : 16 * g + 16] for v, line in zip(inside, lines)]
                 inct[j, b * depth + 16 * g : b * depth + 16 * g + 16, :] = terms[0] + terms[1] + terms[2]
 
+    def weights(j):
+        return tiles[j, 6:7, :] + tiles[j, 7:8, :]
+
     def finish(j):
         sine, loss = sin_and_twice_loss(clo[...])
-        acc[...] += loss * (0.5 * tiles[j, 6:7, :])
+        acc[...] += loss * (0.5 * weights(j))
         wb[j] = jnp.transpose(sine).astype(jnp.bfloat16)
 
-    def send_rows(j):
-        if j < GROUP // 2:
-            for q in range(2):
-                d = 2 * pair(j) + q
-                put(wb.at[j, pl.ds(q * LANES, LANES)], res_ref.at[pl.ds(0, LANES), my_lanes], res_s, res_r, d)
-            return
-
-        @pl.loop(0, GROUP)
-        def _(k):
-            d = peer(k)
-            put(
-                wb.at[j, pl.ds(pl.multiple_of(16 * d, 16), 16)],
-                res_ref.at[pl.ds(LANES, 16), my_lanes], lef_s, res_r, d,
-            )
+    def send_pair(j):
+        for q in range(2):
+            d = 2 * pair(j) + q
+            put(wb.at[j, pl.ds(q * LANES, LANES)], res_ref.at[pl.ds(0, LANES), my_lanes], res_s, res_r, d)
 
     @pl.when(active)
     def _():
@@ -205,33 +199,34 @@
 
         for j in range(GROUP // 2):
             for q in range(2):
-                tiles[j, :, q * LANES : (q + 1) * LANES] = idxs[2 * pair(j) + q, :, 0:LANES]
+                tiles[j, :, q * LANES : (q + 1) * LANES] = idxs[2 * pair(j) + q, :, 0:LANES].astype(jnp.float32)
         for q in range(2):
-            rest = idxs[8 * q, :, LANES:]
+            rest = idxs[8 * q, :, LANES:].astype(jnp.float32)
             for i in range(1, 8):
-                rest = rest + idxs[8 * q + i, :, LANES:]
+                rest = rest + idxs[8 * q + i, :, LANES:].astype(jnp.float32)
             tiles[GROUP // 2, :, q * LANES : (q + 1) * LANES] = rest
-        build(0)
+
+        pl.loop(0, steps)(build)
 
         for half in range(2):
             took(ph.at[pl.ds(8 * half, 8)], ph_r.at[half])
             block = ph[8 * half : 8 * half + 8].reshape(8 * depth, LANES)
             pht[:, 8 * depth * half : 8 * depth * (half + 1)] = jnp.transpose(block.astype(jnp.float32)).astype(jnp.bfloat16)
 
-        for j in range(steps):
+        clo[...] = jnp.dot(pht[...], inct[0], preferred_element_type=jnp.float32)
+
+        @pl.loop(1, steps)
+        def _(j):
             closure = jnp.dot(pht[...], inct[j], preferred_element_type=jnp.float32)
-            if j > 0:
-                finish(j - 1)
-            if j + 1 < steps:
-                build(j + 1)
+            finish(j - 1)
             clo[...] = closure
-            if j > 0:
-                send_rows(j - 1)
+            send_pair(j - 1)
+
         finish(steps - 1)
 
-        total = tiles[0, 6:7, :]
+        total = weights(0)
         for j in range(1, steps):
-            total = total + tiles[j, 6:7, :]
+            total = total + weights(j)
         both = acc[:, 0:LANES] + acc[:, LANES:]
         misfit = jnp.sum(jnp.transpose(both), axis=0, keepdims=True)
         scores[pix] = misfit / jnp.sum(total, axis=1, keepdims=True)
@@ -248,7 +243,13 @@
 
     @pl.when(active)
     def _():
-        send_rows(steps - 1)
+        @pl.loop(0, GROUP)
+        def _(k):
+            d = peer(k)
+            put(
+                wb.at[steps - 1, pl.ds(pl.multiple_of(16 * d, 16), 16)],
+                res_ref.at[pl.ds(LANES, 16), my_lanes], lef_s, res_r, d,
+            )
 
         @pl.loop(0, 4)
         def _(j):
@@ -308,6 +309,17 @@
     everything = jnp.sum(jnp.sum(fin[...], axis=0)[1:2], axis=1, keepdims=True)
     for s in range(12):
         rel_ref[:, s * LANES : (s + 1) * LANES] = fin[s, 0:1] / (everything / all_pixels)
+
+
+def store(*refs):
+    n = len(refs) // 2
+    sems = refs[-1]
+    flat = [r.at[0] if r.shape[0] == 1 else r for r in refs[:n]]
+    copies = [pltpu.make_async_copy(flat[i], refs[n + i], sems.at[i]) for i in range(n)]
+    for copy in copies:
+        copy.start()
+    for copy in copies:
+        copy.wait()
 
 
 def local(phase, incidence, triplet_weight, date_pairs):
@@ -336,13 +348,13 @@
             pltpu.VMEM((2, rows), jnp.int32),
             pltpu.VMEM((triplets, pixel_count), jnp.bfloat16),
             pltpu.VMEM((depth, pixel_count), jnp.bfloat16),
-            pltpu.VMEM((8, 2 * LANES), jnp.float32),
+            pltpu.VMEM((8, 2 * LANES), jnp.bfloat16),
             pltpu.VMEM((LANES, LANES), jnp.float32),
             pltpu.VMEM((8, 2 * LANES), jnp.float32),
             pltpu.VMEM((depth, pixel_count), jnp.bfloat16),
             pltpu.VMEM((GROUP, depth, LANES), jnp.bfloat16),
             pltpu.VMEM((LANES, GROUP * depth), jnp.bfloat16),
-            pltpu.VMEM((GROUP, 8, 2 * LANES), jnp.float32),
+            pltpu.VMEM((GROUP, 8, 2 * LANES), jnp.bfloat16),
             pltpu.VMEM((pairs, 8, 2 * LANES), jnp.float32),
             pltpu.VMEM((pairs, GROUP * depth, 2 * LANES), jnp.bfloat16),
             pltpu.VMEM((depth, 2 * LANES), jnp.bfloat16),
@@ -360,7 +372,18 @@
         ],
         compiler_params=pltpu.CompilerParams(collective_id=0, has_side_effects=True, vmem_limit_bytes=VMEM),
     )(*operands)
-    return (residual, relative.reshape(pixel_count), corrected)
+    return pl.pallas_call(
+        store,
+        out_shape=(
+            jax.ShapeDtypeStruct(residual.shape, jnp.float32),
+            jax.ShapeDtypeStruct((pixel_count,), jnp.float32),
+            jax.ShapeDtypeStruct(corrected.shape, jnp.float32),
+        ),
+        in_specs=[pl.BlockSpec(memory_space=pl.ANY)] * 3,
+        out_specs=[hbm] * 3,
+        scratch_shapes=[pltpu.SemaphoreType.DMA((3,))],
+        compiler_params=pltpu.CompilerParams(vmem_limit_bytes=1024 * 1024),
+    )(residual, relative, corrected)
 
 
 def solution(mesh):

time: 40.6 us -> 38.9 us (0.958)
  local copies, waits for them, and re-layouts: 1.69 us -> 0 us
  other arithmetic: 0.62 us -> 0 us
  Pallas kernels: 37.5 us -> 38.1 us
    unnamed x2 -> x0, local copies, waits for them, and re-layouts: 1.69 us -> none
    pallas_call x0 -> x1, Pallas kernels: none -> 1.1 us  [local(): pl.pallas_call(store, out_shape=(jax.ShapeDtypeStruct(residual.shape, jnp...]
    pallas_call x1 -> x0, other arithmetic: 0.62 us -> none  [local(): pl.pallas_call(functools.partial(kernel, pixes * pixel_count), out_shape=...]
    pallas_call x1, Pallas kernels: 37.5 us -> 37 us  [local(): pl.pallas_call(functools.partial(kernel, pixes * pixel_count), out_shape=...]
where the time goes in v5:
time: 38.9 us; the launch traced here: 38.7 us
  Pallas kernels  38.1 us (98%)
  between operations  0.64 us (2%)
    pallas_call x1, Pallas kernels, local(): pl.pallas_call(functools.partial(kernel, pixes * pixel_count), out_shape=...  37 us
    pallas_call x1, Pallas kernels, local(): pl.pallas_call(store, out_shape=(jax.ShapeDtypeStruct(residual.shape, jnp...  1.1 us

profile of v5, /device:TPU:1, one launch (start us, length us, event | category | flops | bytes accessed | tf_op | source)
XLA Modules:
  0.0 38.7 jit_solution(10471813861081037605)
XLA Ops:
  0.6 37.0 %shard_map.67 = (f32[144,1536]{1,0:T(8,128)S(1)}, f32[1,1536]{1,0:T(1,128)S(1)}, f32[75,1536]{1,0:T(8,128)S(1)}) custom-call(bf16[75,1536]{1,0:T(8,128)(2,1)} %phase_hbm.1, s32[144,1200]{1,0:T(8,128)} %inc_hbm.1, f32[1,144]{1,0:T(1,128)} %bitcast.2, s32[2,75]{1,0:T(2,128)} %bitcast.3), custom_call_target="tpu_custom_call" | custom-call | tf_op jit(solution)/shard_map/pallas_call | solution.py:335
  37.6 1.1 %shard_map.68 = (f32[144,1536]{1,0:T(8,128)}, f32[1536]{0:T(1024)}, f32[75,1536]{1,0:T(8,128)}) custom-call(f32[144,1536]{1,0:T(8,128)S(1)} %get-tuple-element.6.refs_0_, f32[1,1536]{1,0:T(1,128)S(1)} %get-tuple-element.7.refs_1_, f32[75,1536]{1,0:T(8,128)S(1)} %get-tuple-element.8.refs_2_), custom_call_target="tpu_custom_call" | custom-call | tf_op jit(solution)/shard_map/pallas_call | solution.py:375

commit v6 on v5

--- a/solution.py
+++ b/solution.py
@@ -34,14 +34,14 @@
 
 
 def rank_of(device, core):
-    return lax.rem(lax.rem(device, 4) - device // 4 - 2 * core + 7, 4)
+    return lax.rem(lax.rem(device, 4) + device // 4 + 2 * core, 4)
 
 
 def kernel(
     all_pixels,
     phase_hbm, inc_hbm, weight_hbm, dates_hbm, residual_ref, rel_ref, corrected_ref,
     inc, phase, weight, dates, res_ref, cor_ref, idx, rest16, wrow, padded, ph, pht, idxs, tiles, inct, iota, clo, wb, cb, acc, scores, fin_out, fin,
-    in_sem, ph_r, idx_s, idx_r, ph_s, res_s, res_r, lef_s, cor_s, cor_r, fin_s, fin_r, pix_s, pix_r,
+    in_sem, ph_r, idx_r, idx_s, ph_s, res_s, res_r, lef_s, cor_s, cor_r, fin_s, fin_r, pix_s, pix_r,
     near1, near2, near4,
 ):
     me = lax.axis_index("ifg")
@@ -153,7 +153,7 @@
             def _():
                 body(device, pl.multiple_of((3 * (device // 4) + their) * LANES, LANES))
 
-    to_shares(lambda d, at: put(idx, idxs.at[me], idx_s, idx_r, d))
+    to_shares(lambda d, at: put(idx, idxs.at[me], idx_s, idx_r.at[me // 2], d))
     to_shares(lambda d, at: put(padded.at[:, pl.ds(at, LANES)], ph.at[me], ph_s, ph_r.at[me // 8], d))
 
     pl.semaphore_wait(near1, 2)
@@ -183,10 +183,13 @@
     def weights(j):
         return tiles[j, 6:7, :] + tiles[j, 7:8, :]
 
-    def finish(j):
-        sine, loss = sin_and_twice_loss(clo[...])
-        acc[...] += loss * (0.5 * weights(j))
-        wb[j] = jnp.transpose(sine).astype(jnp.bfloat16)
+    def finish(j, count):
+        lost = acc[...]
+        for q in range(count):
+            sine, loss = sin_and_twice_loss(clo[q])
+            lost = lost + loss * (0.5 * weights(j + q))
+            wb[j + q] = jnp.transpose(sine).astype(jnp.bfloat16)
+        acc[...] = lost
 
     def send_pair(j):
         for q in range(2):
@@ -195,34 +198,48 @@
 
     @pl.when(active)
     def _():
-        took(idxs, idx_r)
-
-        for j in range(GROUP // 2):
+        @pl.loop(0, GROUP // 2)
+        def _(j):
+            p = pair(j)
+            took(idxs.at[pl.ds(2 * p, 2)], idx_r.at[p])
             for q in range(2):
-                tiles[j, :, q * LANES : (q + 1) * LANES] = idxs[2 * pair(j) + q, :, 0:LANES].astype(jnp.float32)
+                tiles[j, :, q * LANES : (q + 1) * LANES] = idxs[2 * p + q, :, 0:LANES].astype(jnp.float32)
+            build(j)
+
         for q in range(2):
             rest = idxs[8 * q, :, LANES:].astype(jnp.float32)
             for i in range(1, 8):
                 rest = rest + idxs[8 * q + i, :, LANES:].astype(jnp.float32)
             tiles[GROUP // 2, :, q * LANES : (q + 1) * LANES] = rest
 
-        pl.loop(0, steps)(build)
+        build(steps - 1)
 
         for half in range(2):
             took(ph.at[pl.ds(8 * half, 8)], ph_r.at[half])
             block = ph[8 * half : 8 * half + 8].reshape(8 * depth, LANES)
             pht[:, 8 * depth * half : 8 * depth * (half + 1)] = jnp.transpose(block.astype(jnp.float32)).astype(jnp.bfloat16)
 
-        clo[...] = jnp.dot(pht[...], inct[0], preferred_element_type=jnp.float32)
-
-        @pl.loop(1, steps)
-        def _(j):
-            closure = jnp.dot(pht[...], inct[j], preferred_element_type=jnp.float32)
-            finish(j - 1)
-            clo[...] = closure
-            send_pair(j - 1)
-
-        finish(steps - 1)
+        def multiply(j):
+            return jnp.dot(pht[...], inct[j], preferred_element_type=jnp.float32)
+
+        for q in range(2):
+            clo[q] = multiply(q)
+
+        @pl.loop(1, GROUP // 4)
+        def _(g):
+            closure = [multiply(2 * g + q) for q in range(2)]
+            finish(2 * g - 2, 2)
+            for q in range(2):
+                clo[q] = closure[q]
+            for q in range(2):
+                send_pair(2 * g - 2 + q)
+
+        closure = multiply(steps - 1)
+        finish(steps - 3, 2)
+        clo[0] = closure
+        for q in range(2):
+            send_pair(steps - 3 + q)
+        finish(steps - 1, 1)
 
         total = weights(0)
         for j in range(1, steps):
@@ -358,7 +375,7 @@
             pltpu.VMEM((pairs, 8, 2 * LANES), jnp.float32),
             pltpu.VMEM((pairs, GROUP * depth, 2 * LANES), jnp.bfloat16),
             pltpu.VMEM((depth, 2 * LANES), jnp.bfloat16),
-            pltpu.VMEM((LANES, 2 * LANES), jnp.float32),
+            pltpu.VMEM((2, LANES, 2 * LANES), jnp.float32),
             pltpu.VMEM((pairs, 2 * LANES, LANES), jnp.bfloat16),
             pltpu.VMEM((GROUP, depth, LANES), jnp.bfloat16),
             pltpu.VMEM((LANES, 2 * LANES), jnp.float32),
@@ -367,7 +384,8 @@
             pltpu.VMEM((GROUP, 2, LANES), jnp.float32),
             pltpu.SemaphoreType.DMA((4,)),
             pltpu.SemaphoreType.DMA((2,)),
-            *[pltpu.SemaphoreType.DMA] * 12,
+            pltpu.SemaphoreType.DMA((GROUP // 2,)),
+            *[pltpu.SemaphoreType.DMA] * 11,
             *[pltpu.SemaphoreType.REGULAR] * 3,
         ],
         compiler_params=pltpu.CompilerParams(collective_id=0, has_side_effects=True, vmem_limit_bytes=VMEM),

time: 38.9 us -> 38.3 us (0.985)
  Pallas kernels: 38.1 us -> 37.5 us
    pallas_call x1, Pallas kernels: 37 us -> 36.4 us  [local(): pl.pallas_call(functools.partial(kernel, pixes * pixel_count), out_shape=...]
where the time goes in v6:
time: 38.3 us; the launch traced here: 38.2 us
  Pallas kernels  37.5 us (98%)
  between operations  0.64 us (2%)
    pallas_call x1, Pallas kernels, local(): pl.pallas_call(functools.partial(kernel, pixes * pixel_count), out_shape=...  36.4 us
    pallas_call x1, Pallas kernels, local(): pl.pallas_call(store, out_shape=(jax.ShapeDtypeStruct(residual.shape, jnp...  1.1 us

profile of v6, /device:TPU:1, one launch (start us, length us, event | category | flops | bytes accessed | tf_op | source)
XLA Modules:
  0.0 38.2 jit_solution(12339629929207309691)
XLA Ops:
  0.6 36.4 %shard_map.67 = (f32[144,1536]{1,0:T(8,128)S(1)}, f32[1,1536]{1,0:T(1,128)S(1)}, f32[75,1536]{1,0:T(8,128)S(1)}) custom-call(bf16[75,1536]{1,0:T(8,128)(2,1)} %phase_hbm.1, s32[144,1200]{1,0:T(8,128)} %inc_hbm.1, f32[1,144]{1,0:T(1,128)} %bitcast.2, s32[2,75]{1,0:T(2,128)} %bitcast.3), custom_call_target="tpu_custom_call" | custom-call | tf_op jit(solution)/shard_map/pallas_call | solution.py:352
  37.1 1.1 %shard_map.68 = (f32[144,1536]{1,0:T(8,128)}, f32[1536]{0:T(1024)}, f32[75,1536]{1,0:T(8,128)}) custom-call(f32[144,1536]{1,0:T(8,128)S(1)} %get-tuple-element.6.refs_0_, f32[1,1536]{1,0:T(1,128)S(1)} %get-tuple-element.7.refs_1_, f32[75,1536]{1,0:T(8,128)S(1)} %get-tuple-element.8.refs_2_), custom_call_target="tpu_custom_call" | custom-call | tf_op jit(solution)/shard_map/pallas_call | solution.py:393

commit v7 on v6

--- a/solution.py
+++ b/solution.py
@@ -9,6 +9,7 @@
 
 GROUP = 16
 LANES = 128
+EARLY = 2
 VMEM = 16 * 1024 * 1024
 INV_2PI = 0.15915494309189535
 TWO_PI_HI = 6.28125
@@ -31,6 +32,12 @@
     sine = r + (r * z) * poly(SIN, z)
     cosine = 1.0 + z * poly(COS, z)
     return sine * cosine, sine * sine
+
+
+PEERS = sorted(
+    ((dx, dy) for dx in range(4) for dy in range(4) if dx or dy),
+    key=lambda p: -min(p[0], 4 - p[0]) - min(p[1], 4 - p[1]),
+)
 
 
 def rank_of(device, core):
@@ -57,11 +64,14 @@
     pixes = scores.shape[0]
     steps = GROUP // 2 + 1
 
-    def peer(j):
-        return 4 * lax.rem(x + j // 4 + 2, 4) + lax.rem(y + lax.rem(j, 4) + 2, 4)
+    def peer(dx, dy):
+        return xs[dx] + ys[dy]
+
+    xs = [4 * lax.rem(x + i, 4) for i in range(4)]
+    ys = [lax.rem(y + i, 4) for i in range(4)]
 
     def far(k):
-        return lax.rem(pix + pixes // 2 + (k + 1) // 2 * (1 - 2 * lax.rem(k, 2)), pixes)
+        return lax.rem(pix + pixes // 2 + (k + 1) // 2 * (1 - 2 * (k % 2)), pixes)
 
     barrier = pltpu.get_barrier_semaphore()
 
@@ -129,40 +139,42 @@
     tell_along_z(near1, 1)
 
     def put(src, dst, send, recv, device):
-        @pl.when(device != me)
-        def _():
-            pltpu.make_async_remote_copy(
-                src_ref=src, dst_ref=dst, send_sem=send, recv_sem=recv,
-                device_id={"ifg": device}, device_id_type=pl.DeviceIdType.MESH,
-            ).start()
-
-        @pl.when(device == me)
-        def _():
-            pltpu.make_async_copy(src, dst, recv).start()
+        pltpu.make_async_remote_copy(
+            src_ref=src, dst_ref=dst, send_sem=send, recv_sem=recv,
+            device_id={"ifg": device}, device_id_type=pl.DeviceIdType.MESH,
+        ).start()
+
+    def keep(src, dst, recv):
+        pltpu.make_async_copy(src, dst, recv).start()
 
     def took(ref, sem):
         pltpu.make_async_copy(ref, ref, sem).wait()
 
-    def to_shares(body):
-        @pl.loop(0, GROUP)
-        def _(j):
-            device = peer(j)
-            their = rank_of(device, core)
+    def to_shares(body, own):
+        for e in (0, 1, 3, 2):
+            their = lax.rem(x + y + 2 * core + e, 4)
 
             @pl.when(their < 3)
             def _():
-                body(device, pl.multiple_of((3 * (device // 4) + their) * LANES, LANES))
-
-    to_shares(lambda d, at: put(idx, idxs.at[me], idx_s, idx_r.at[me // 2], d))
-    to_shares(lambda d, at: put(padded.at[:, pl.ds(at, LANES)], ph.at[me], ph_s, ph_r.at[me // 8], d))
-
+                for dx, dy in PEERS:
+                    if (dx + dy) % 4 == e:
+                        at = pl.multiple_of((3 * lax.rem(x + dx, 4) + their) * LANES, LANES)
+                        body(peer(dx, dy), at)
+                if e == 0:
+                    own()
+
+    here_idx = idx_r.at[me // 2]
+    here_ph = ph_r.at[me // 8]
+    to_shares(lambda d, at: put(idx, idxs.at[me], idx_s, here_idx, d), lambda: keep(idx, idxs.at[me], here_idx))
     pl.semaphore_wait(near1, 2)
     tell_along_z(near2, 2)
-    pl.semaphore_wait(near2, 2)
-    tell_along_z(near4, 4)
+    to_shares(
+        lambda d, at: put(padded.at[:, pl.ds(at, LANES)], ph.at[me], ph_s, here_ph, d),
+        lambda: keep(padded.at[:, my_lanes], ph.at[me], here_ph),
+    )
 
     def pair(j):
-        return lax.rem(me // 2 + j, GROUP // 2)
+        return lax.rem(me // 2 + 1 + j, GROUP // 2)
 
     def build(j):
         t = tiles[j]
@@ -191,20 +203,38 @@
             wb[j + q] = jnp.transpose(sine).astype(jnp.bfloat16)
         acc[...] = lost
 
+    mine = res_ref.at[pl.ds(0, LANES), my_lanes]
+    mine16 = res_ref.at[pl.ds(LANES, 16), my_lanes]
+
     def send_pair(j):
         for q in range(2):
-            d = 2 * pair(j) + q
-            put(wb.at[j, pl.ds(q * LANES, LANES)], res_ref.at[pl.ds(0, LANES), my_lanes], res_s, res_r, d)
+            put(wb.at[j, pl.ds(q * LANES, LANES)], mine, res_s, res_r, 2 * pair(j) + q)
+
+    def send_own_pair(j):
+        odd = lax.rem(me, 2)
+        own = pl.ds(pl.multiple_of(odd * LANES, LANES), LANES)
+        next_door = pl.ds(pl.multiple_of((1 - odd) * LANES, LANES), LANES)
+        put(wb.at[j, next_door], mine, res_s, res_r, me + 1 - 2 * odd)
+        keep(wb.at[j, own], mine, res_r)
+
+    @pl.when(rank == 3)
+    def _():
+        pl.semaphore_wait(near2, 2)
+        tell_along_z(near4, 4)
 
     @pl.when(active)
     def _():
-        @pl.loop(0, GROUP // 2)
-        def _(j):
+        def arrived(j):
             p = pair(j)
             took(idxs.at[pl.ds(2 * p, 2)], idx_r.at[p])
             for q in range(2):
                 tiles[j, :, q * LANES : (q + 1) * LANES] = idxs[2 * p + q, :, 0:LANES].astype(jnp.float32)
             build(j)
+
+        pl.loop(0, EARLY)(arrived)
+        pl.semaphore_wait(near2, 2)
+        tell_along_z(near4, 4)
+        pl.loop(EARLY, GROUP // 2)(arrived)
 
         for q in range(2):
             rest = idxs[8 * q, :, LANES:].astype(jnp.float32)
@@ -237,8 +267,8 @@
         closure = multiply(steps - 1)
         finish(steps - 3, 2)
         clo[0] = closure
-        for q in range(2):
-            send_pair(steps - 3 + q)
+        send_pair(steps - 3)
+        send_own_pair(steps - 2)
         finish(steps - 1, 1)
 
         total = weights(0)
@@ -250,23 +280,20 @@
 
     pl.semaphore_wait(near4, 2)
 
-    @pl.loop(0, pixes - 1)
-    def _(k):
-        other = far(k)
+    for k in range(pixes - 1):
         pltpu.make_async_remote_copy(
             src_ref=scores.at[pix], dst_ref=scores.at[pix], send_sem=pix_s, recv_sem=pix_r,
-            device_id={"pix": other}, device_id_type=pl.DeviceIdType.MESH,
+            device_id={"pix": far(k)}, device_id_type=pl.DeviceIdType.MESH,
         ).start()
 
     @pl.when(active)
     def _():
-        @pl.loop(0, GROUP)
-        def _(k):
-            d = peer(k)
-            put(
-                wb.at[steps - 1, pl.ds(pl.multiple_of(16 * d, 16), 16)],
-                res_ref.at[pl.ds(LANES, 16), my_lanes], lef_s, res_r, d,
-            )
+        def sixteen(d):
+            return wb.at[steps - 1, pl.ds(pl.multiple_of(16 * d, 16), 16)]
+
+        for dx, dy in PEERS:
+            put(sixteen(peer(dx, dy)), mine16, lef_s, res_r, peer(dx, dy))
+        keep(sixteen(me), mine16, res_r)
 
         @pl.loop(0, 4)
         def _(j):
@@ -278,7 +305,14 @@
             cb[pl.ds(4 * c, 4)] = corr.astype(jnp.bfloat16).reshape(4, depth, LANES)
             for q in range(4):
                 d = 4 * c + q
-                put(cb.at[d], cor_ref.at[:, my_lanes], cor_s, cor_r, d)
+
+                @pl.when(d != me)
+                def _():
+                    put(cb.at[d], cor_ref.at[:, my_lanes], cor_s, cor_r, d)
+
+                @pl.when(d == me)
+                def _():
+                    keep(cb.at[d], cor_ref.at[:, my_lanes], cor_r)
 
     took(scores.at[pl.ds(0, pixes - 1)], pix_r)
 
@@ -286,10 +320,9 @@
     fin_out[1:2] = jnp.sum(scores[...], axis=0)
     slot = jnp.where(active, share, 12 + x)
 
-    @pl.loop(0, GROUP)
-    def _(k):
-        d = peer(k)
-        put(fin_out, fin.at[slot], fin_s, fin_r, d)
+    for dx, dy in PEERS:
+        put(fin_out, fin.at[slot], fin_s, fin_r, peer(dx, dy))
+    keep(fin_out, fin.at[slot], fin_r)
 
     others = GROUP - 1
     took(scores.at[pl.ds(0, pixes - 1)], pix_s)
@@ -328,11 +361,13 @@
         rel_ref[:, s * LANES : (s + 1) * LANES] = fin[s, 0:1] / (everything / all_pixels)
 
 
-def store(*refs):
-    n = len(refs) // 2
-    sems = refs[-1]
-    flat = [r.at[0] if r.shape[0] == 1 else r for r in refs[:n]]
-    copies = [pltpu.make_async_copy(flat[i], refs[n + i], sems.at[i]) for i in range(n)]
+def store(residual, relative, corrected, residual_out, relative_out, corrected_out, sems):
+    copies = [(relative.at[0], relative_out)]
+    for src, dst, step in ((residual, residual_out, 48), (corrected, corrected_out, 40)):
+        for at in range(0, src.shape[0], step):
+            rows = pl.ds(at, min(step, src.shape[0] - at))
+            copies.append((src.at[rows], dst.at[rows]))
+    copies = [pltpu.make_async_copy(src, dst, sems.at[i]) for i, (src, dst) in enumerate(copies)]
     for copy in copies:
         copy.start()
     for copy in copies:
@@ -399,7 +434,7 @@
         ),
         in_specs=[pl.BlockSpec(memory_space=pl.ANY)] * 3,
         out_specs=[hbm] * 3,
-        scratch_shapes=[pltpu.SemaphoreType.DMA((3,))],
+        scratch_shapes=[pltpu.SemaphoreType.DMA((6,))],
         compiler_params=pltpu.CompilerParams(vmem_limit_bytes=1024 * 1024),
     )(residual, relative, corrected)
 

time: 38.3 us -> 38.3 us (level)
  no operation moved by 1% of the time
where the time goes in v7:
time: 38.3 us; the launch traced here: 38.2 us
  Pallas kernels  37.5 us (98%)
  between operations  0.64 us (2%)
    pallas_call x1, Pallas kernels, local(): pl.pallas_call(functools.partial(kernel, pixes * pixel_count), out_shape=...  36.4 us
    pallas_call x1, Pallas kernels, local(): pl.pallas_call(store, out_shape=(jax.ShapeDtypeStruct(residual.shape, jnp...  1.12 us

profile of v7, /device:TPU:1, one launch (start us, length us, event | category | flops | bytes accessed | tf_op | source)
XLA Modules:
  0.0 38.2 jit_solution(10940485041340011851)
XLA Ops:
  0.6 36.4 %shard_map.67 = (f32[144,1536]{1,0:T(8,128)S(1)}, f32[1,1536]{1,0:T(1,128)S(1)}, f32[75,1536]{1,0:T(8,128)S(1)}) custom-call(bf16[75,1536]{1,0:T(8,128)(2,1)} %phase_hbm.1, s32[144,1200]{1,0:T(8,128)} %inc_hbm.1, f32[1,144]{1,0:T(1,128)} %bitcast.2, s32[2,75]{1,0:T(2,128)} %bitcast.3), custom_call_target="tpu_custom_call" | custom-call | tf_op jit(solution)/shard_map/pallas_call | solution.py:387
  37.0 1.1 %shard_map.68 = (f32[144,1536]{1,0:T(8,128)}, f32[1536]{0:T(1024)}, f32[75,1536]{1,0:T(8,128)}) custom-call(f32[144,1536]{1,0:T(8,128)S(1)} %get-tuple-element.6.residual, f32[1,1536]{1,0:T(1,128)S(1)} %get-tuple-element.7.relative, f32[75,1536]{1,0:T(8,128)S(1)} %get-tuple-element.8.corrected), custom_call_target="tpu_custom_call" | custom-call | tf_op jit(solution)/shard_map/pallas_call | solution.py:428

commit v8 on v7

--- a/solution.py
+++ b/solution.py
@@ -75,9 +75,6 @@
 
     barrier = pltpu.get_barrier_semaphore()
 
-    def tell_group(k):
-        pl.semaphore_signal(barrier, inc=1, device_id={"ifg": lax.rem(me + k, GROUP)}, device_id_type=pl.DeviceIdType.MESH)
-
     def tell_pix(sem, other):
         pl.semaphore_signal(sem, inc=1, device_id={"pix": lax.rem(other, pixes)}, device_id_type=pl.DeviceIdType.MESH)
 
@@ -85,6 +82,13 @@
         tell_pix(sem, pix + 2 * distance)
         tell_pix(sem, pix + pixes - 2 * distance)
 
+    for dx, dy in PEERS:
+        pl.semaphore_signal(barrier, inc=1, device_id={"ifg": peer(dx, dy)}, device_id_type=pl.DeviceIdType.MESH)
+    across = 2 * (pix // 2) + 1 - core
+    tell_pix(barrier, across)
+    tell_along_z(barrier, 1)
+    tell_pix(barrier, across + 2)
+    tell_pix(barrier, across + pixes - 2)
     read_inc = pltpu.make_async_copy(inc_hbm, inc, in_sem.at[0])
     read_inc.start()
     read_phase = pltpu.make_async_copy(phase_hbm, phase, in_sem.at[1])
@@ -93,12 +97,6 @@
     read_weight.start()
     read_dates = pltpu.make_async_copy(dates_hbm, dates, in_sem.at[3])
     read_dates.start()
-    pl.loop(1, GROUP)(tell_group)
-    across = 2 * (pix // 2) + 1 - core
-    tell_pix(barrier, across)
-    tell_along_z(barrier, 1)
-    tell_pix(barrier, across + 2)
-    tell_pix(barrier, across + pixes - 2)
 
     iota[...] = lax.broadcasted_iota(jnp.int32, iota.shape, 0).astype(jnp.float32).astype(jnp.bfloat16)
     acc[...] = jnp.zeros_like(acc)
@@ -224,8 +222,9 @@
 
     @pl.when(active)
     def _():
-        def arrived(j):
-            p = pair(j)
+        def arrived(k):
+            p = lax.rem(k + 1, GROUP // 2)
+            j = lax.rem(p - me // 2 + GROUP // 2 - 1, GROUP // 2)
             took(idxs.at[pl.ds(2 * p, 2)], idx_r.at[p])
             for q in range(2):
                 tiles[j, :, q * LANES : (q + 1) * LANES] = idxs[2 * p + q, :, 0:LANES].astype(jnp.float32)
@@ -267,8 +266,6 @@
         closure = multiply(steps - 1)
         finish(steps - 3, 2)
         clo[0] = closure
-        send_pair(steps - 3)
-        send_own_pair(steps - 2)
         finish(steps - 1, 1)
 
         total = weights(0)
@@ -288,6 +285,9 @@
 
     @pl.when(active)
     def _():
+        send_pair(steps - 3)
+        send_own_pair(steps - 2)
+
         def sixteen(d):
             return wb.at[steps - 1, pl.ds(pl.multiple_of(16 * d, 16), 16)]
 

time: 38.3 us -> 38.3 us (level)
  no operation moved by 1% of the time
where the time goes in v8:
time: 38.3 us; the launch traced here: 38.1 us
  Pallas kernels  37.5 us (98%)
  between operations  0.64 us (2%)
    pallas_call x1, Pallas kernels, local(): pl.pallas_call(functools.partial(kernel, pixes * pixel_count), out_shape=...  36.4 us
    pallas_call x1, Pallas kernels, local(): pl.pallas_call(store, out_shape=(jax.ShapeDtypeStruct(residual.shape, jnp...  1.12 us

profile of v8, /device:TPU:1, one launch (start us, length us, event | category | flops | bytes accessed | tf_op | source)
XLA Modules:
  0.0 38.1 jit_solution(16436508448178190554)
XLA Ops:
  0.6 36.4 %shard_map.67 = (f32[144,1536]{1,0:T(8,128)S(1)}, f32[1,1536]{1,0:T(1,128)S(1)}, f32[75,1536]{1,0:T(8,128)S(1)}) custom-call(bf16[75,1536]{1,0:T(8,128)(2,1)} %phase_hbm.1, s32[144,1200]{1,0:T(8,128)} %inc_hbm.1, f32[1,144]{1,0:T(1,128)} %bitcast.2, s32[2,75]{1,0:T(2,128)} %bitcast.3), custom_call_target="tpu_custom_call" | custom-call | tf_op jit(solution)/shard_map/pallas_call | solution.py:387
  37.0 1.1 %shard_map.68 = (f32[144,1536]{1,0:T(8,128)}, f32[1536]{0:T(1024)}, f32[75,1536]{1,0:T(8,128)}) custom-call(f32[144,1536]{1,0:T(8,128)S(1)} %get-tuple-element.6.residual, f32[1,1536]{1,0:T(1,128)S(1)} %get-tuple-element.7.relative, f32[75,1536]{1,0:T(8,128)S(1)} %get-tuple-element.8.corrected), custom_call_target="tpu_custom_call" | custom-call | tf_op jit(solution)/shard_map/pallas_call | solution.py:428

commit v9 on v8

--- a/solution.py
+++ b/solution.py
@@ -41,7 +41,8 @@
 
 
 def rank_of(device, core):
-    return lax.rem(lax.rem(device, 4) + device // 4 + 2 * core, 4)
+    x, y = device // 4, lax.rem(device, 4)
+    return lax.rem(jnp.where(core == 0, y + x, y - x + 7), 4)
 
 
 def kernel(
@@ -149,13 +150,13 @@
         pltpu.make_async_copy(ref, ref, sem).wait()
 
     def to_shares(body, own):
-        for e in (0, 1, 3, 2):
-            their = lax.rem(x + y + 2 * core + e, 4)
-
-            @pl.when(their < 3)
+        for c, e in ((c, e) for c in range(2) for e in (0, 1, 3, 2)):
+            their = lax.rem(rank + e, 4)
+
+            @pl.when(jnp.logical_and(core == c, their < 3))
             def _():
                 for dx, dy in PEERS:
-                    if (dx + dy) % 4 == e:
+                    if (dy + dx * (1 - 2 * c)) % 4 == e:
                         at = pl.multiple_of((3 * lax.rem(x + dx, 4) + their) * LANES, LANES)
                         body(peer(dx, dy), at)
                 if e == 0:

time: 38.3 us -> 37.9 us (0.990)
  no operation moved by 1% of the time
where the time goes in v9:
time: 37.9 us; the launch traced here: 37.8 us
  Pallas kernels  37.2 us (98%)
  between operations  0.64 us (2%)
    pallas_call x1, Pallas kernels, local(): pl.pallas_call(functools.partial(kernel, pixes * pixel_count), out_shape=...  36 us
    pallas_call x1, Pallas kernels, local(): pl.pallas_call(store, out_shape=(jax.ShapeDtypeStruct(residual.shape, jnp...  1.12 us

profile of v9, /device:TPU:1, one launch (start us, length us, event | category | flops | bytes accessed | tf_op | source)
XLA Modules:
  0.0 37.8 jit_solution(18269476303584121778)
XLA Ops:
  0.6 36.0 %shard_map.67 = (f32[144,1536]{1,0:T(8,128)S(1)}, f32[1,1536]{1,0:T(1,128)S(1)}, f32[75,1536]{1,0:T(8,128)S(1)}) custom-call(bf16[75,1536]{1,0:T(8,128)(2,1)} %phase_hbm.1, s32[144,1200]{1,0:T(8,128)} %inc_hbm.1, f32[1,144]{1,0:T(1,128)} %bitcast.2, s32[2,75]{1,0:T(2,128)} %bitcast.3), custom_call_target="tpu_custom_call" | custom-call | tf_op jit(solution)/shard_map/pallas_call | solution.py:388
  36.7 1.1 %shard_map.68 = (f32[144,1536]{1,0:T(8,128)}, f32[1536]{0:T(1024)}, f32[75,1536]{1,0:T(8,128)}) custom-call(f32[144,1536]{1,0:T(8,128)S(1)} %get-tuple-element.6.residual, f32[1,1536]{1,0:T(1,128)S(1)} %get-tuple-element.7.relative, f32[75,1536]{1,0:T(8,128)S(1)} %get-tuple-element.8.corrected), custom_call_target="tpu_custom_call" | custom-call | tf_op jit(solution)/shard_map/pallas_call | solution.py:429

commit v10 on v9

--- a/solution.py
+++ b/solution.py
@@ -83,6 +83,8 @@
         tell_pix(sem, pix + 2 * distance)
         tell_pix(sem, pix + pixes - 2 * distance)
 
+    read_inc = pltpu.make_async_copy(inc_hbm, inc, in_sem.at[0])
+    read_inc.start()
     for dx, dy in PEERS:
         pl.semaphore_signal(barrier, inc=1, device_id={"ifg": peer(dx, dy)}, device_id_type=pl.DeviceIdType.MESH)
     across = 2 * (pix // 2) + 1 - core
@@ -90,8 +92,6 @@
     tell_along_z(barrier, 1)
     tell_pix(barrier, across + 2)
     tell_pix(barrier, across + pixes - 2)
-    read_inc = pltpu.make_async_copy(inc_hbm, inc, in_sem.at[0])
-    read_inc.start()
     read_phase = pltpu.make_async_copy(phase_hbm, phase, in_sem.at[1])
     read_phase.start()
     read_weight = pltpu.make_async_copy(weight_hbm, weight, in_sem.at[2])
@@ -364,7 +364,7 @@
 
 def store(residual, relative, corrected, residual_out, relative_out, corrected_out, sems):
     copies = [(relative.at[0], relative_out)]
-    for src, dst, step in ((residual, residual_out, 48), (corrected, corrected_out, 40)):
+    for src, dst, step in ((residual, residual_out, 144), (corrected, corrected_out, 80)):
         for at in range(0, src.shape[0], step):
             rows = pl.ds(at, min(step, src.shape[0] - at))
             copies.append((src.at[rows], dst.at[rows]))
@@ -435,7 +435,7 @@
         ),
         in_specs=[pl.BlockSpec(memory_space=pl.ANY)] * 3,
         out_specs=[hbm] * 3,
-        scratch_shapes=[pltpu.SemaphoreType.DMA((6,))],
+        scratch_shapes=[pltpu.SemaphoreType.DMA((3,))],
         compiler_params=pltpu.CompilerParams(vmem_limit_bytes=1024 * 1024),
     )(residual, relative, corrected)
 

time: 37.9 us -> 37.9 us (level)
  no operation moved by 1% of the time
where the time goes in v10:
time: 37.9 us; the launch traced here: 37.8 us
  Pallas kernels  37.1 us (98%)
  between operations  0.64 us (2%)
    pallas_call x1, Pallas kernels, local(): pl.pallas_call(functools.partial(kernel, pixes * pixel_count), out_shape=...  36 us
    pallas_call x1, Pallas kernels, local(): pl.pallas_call(store, out_shape=(jax.ShapeDtypeStruct(residual.shape, jnp...  1.1 us

profile of v10, /device:TPU:1, one launch (start us, length us, event | category | flops | bytes accessed | tf_op | source)
XLA Modules:
  0.0 37.8 jit_solution(12107797264359262521)
XLA Ops:
  0.6 36.0 %shard_map.67 = (f32[144,1536]{1,0:T(8,128)S(1)}, f32[1,1536]{1,0:T(1,128)S(1)}, f32[75,1536]{1,0:T(8,128)S(1)}) custom-call(bf16[75,1536]{1,0:T(8,128)(2,1)} %phase_hbm.1, s32[144,1200]{1,0:T(8,128)} %inc_hbm.1, f32[1,144]{1,0:T(1,128)} %bitcast.2, s32[2,75]{1,0:T(2,128)} %bitcast.3), custom_call_target="tpu_custom_call" | custom-call | tf_op jit(solution)/shard_map/pallas_call | solution.py:388
  36.7 1.1 %shard_map.68 = (f32[144,1536]{1,0:T(8,128)}, f32[1536]{0:T(1024)}, f32[75,1536]{1,0:T(8,128)}) custom-call(f32[144,1536]{1,0:T(8,128)S(1)} %get-tuple-element.6.residual, f32[1,1536]{1,0:T(1,128)S(1)} %get-tuple-element.7.relative, f32[75,1536]{1,0:T(8,128)S(1)} %get-tuple-element.8.corrected), custom_call_target="tpu_custom_call" | custom-call | tf_op jit(solution)/shard_map/pallas_call | solution.py:429
